TPU v7x, 128 devices: a whole 4x4x4 slice. The times are simulated.
128 devices in a mesh: row: 8 (over x, z_hi), col: 16 (over z_lo, y, core).
Axes of the slice: x: 4, y: 4, z: 4 (z_hi: 2, z_lo: 2; z = z_hi * 2 + z_lo), core: 2. Of those that a mesh axis runs over, the one named last changes fastest.
Arguments:
- covariance: float32 [16384, 16384], P('row', 'col'), may hold values from -1 to 560
- seed_index: int32 [128], replicated, may hold values from 0 to 16383, as said below
Outputs:
- basis: float32 [16384, 384], P('row')
- projection: float32 [384, 256], replicated
- first_pass: float32 [384, 256], replicated
Inputs may be any that keep to these rules, and one draw needn't show every extreme that they name: `seed_index`: 128 distinct column indices.
All inputs are finite; a program needn't handle non-finite values.
Results may differ from a plain program's by a relative error of at most 0.00019.
Values sent between devices are 32-bit elements; how exact they have to be, the bound alone decides.
A program may use at most 128 MiB of HBM per device.

v0:
```python
import jax
import jax.numpy as jnp
from jax import lax
from jax.sharding import PartitionSpec as P

N = 16384
ITERS = 2


def picked_2(value, axis, root):
    return lax.dynamic_index_in_dim(lax.all_gather(value, axis), root, 0, keepdims=False)


def cut_along(value, dim, devices):
    shape = value.shape
    parts = value.reshape(*shape[:dim], devices, shape[dim] // devices, *shape[dim + 1 :])
    return jnp.moveaxis(parts, dim, 0)


def sent_and_summed(value, axis, dim):
    devices = lax.axis_size(axis)
    parts = lax.all_to_all(cut_along(value, dim, devices), axis, 0, 0, tiled=True)
    return jnp.sum(parts, axis=0)


def rows_for(lines, devices):
    spare = -lines.shape[0] % devices
    if not spare:
        return lines
    return jnp.concatenate([lines, jnp.zeros((spare, *lines.shape[1:]), lines.dtype)])


def laid_out(parts, dim):
    shape = list(parts.shape[1:])
    shape[dim] *= parts.shape[0]
    return jnp.moveaxis(parts, 0, dim).reshape(shape)


def copy_for_each(value, axis):
    copies = jnp.broadcast_to(value, (lax.axis_size(axis), *value.shape))
    return lax.all_to_all(copies, axis, split_axis=0, concat_axis=0, tiled=True)


def collect(value, axis, dim):
    return laid_out(copy_for_each(value, axis), dim)


def total_of(value, axes):
    lines = value.reshape(-1, value.shape[-1])
    own = sent_and_summed(rows_for(lines, lax.axis_size(axes)), axes, 0)
    whole = collect(own, axes, 0)
    return whole[: len(lines)].reshape(value.shape)


def taken_together(value, axis):
    return copy_for_each(value, axis).sum(axis=0)


def together(arrays, axis):
    ends = [0]
    for a in arrays:
        ends.append(ends[-1] + a.size)
    subtotal = taken_together(jnp.concatenate([a.ravel() for a in arrays]), axis)
    return tuple((subtotal[b:e].reshape(a.shape) for a, b, e in zip(arrays, ends, ends[1:])))


def product(left, right):
    return jnp.dot(left, right, precision=lax.Precision.HIGHEST, preferred_element_type=jnp.float32)


def finish_block(block, gram):
    lower = jnp.linalg.cholesky(gram)
    basis_block = jax.scipy.linalg.solve_triangular(lower, block.T, lower=True).T
    return (basis_block, lower.T)


def transpose_block(current, col_place, col_count):
    ratio = lax.axis_size("col") // lax.axis_size("row")
    owned = picked_2(current, "row", col_place // ratio)
    vector = lax.dynamic_slice_in_dim(owned, col_place % ratio * col_count, col_count, 0)
    return vector


def local(covariance, seed_index):
    col_count = covariance.shape[1]
    width = seed_index.shape[0]
    col_place = lax.axis_index("col")
    offsets = seed_index - col_place * col_count
    inside = (offsets >= 0) & (offsets < col_count)
    picked = jnp.take(covariance, jnp.clip(offsets, 0, col_count - 1), axis=1)
    start = total_of(jnp.where(inside[None, :], picked, 0.0), "col")
    gram = taken_together(product(start.T, start), "row")
    current, upper = finish_block(start, gram)
    full = current
    blocks = [current]
    projection = jnp.zeros(((ITERS + 1) * width, ITERS * width), jnp.float32)
    first_pass = jnp.zeros(((ITERS + 1) * width, ITERS * width), jnp.float32)
    for section in range(ITERS):
        vector = transpose_block(full, col_place, col_count)
        partial_value = product(covariance, vector)
        stacked = jnp.concatenate(blocks, axis=1)
        image = total_of(partial_value, "col")
        first = taken_together(product(stacked.T, image), "row")
        once = image - product(stacked, first)
        second, raw_gram = together((product(stacked.T, once), product(once.T, once)), "row")
        twice = once - product(stacked, second)
        gram = raw_gram - product(second.T, second)
        current, upper = finish_block(twice, gram)
        projection = projection.at[
            : (section + 1) * width, section * width : (section + 1) * width
        ].set(first + second)
        projection = projection.at[
            (section + 1) * width : (section + 2) * width, section * width : (section + 1) * width
        ].set(upper)
        first_pass = first_pass.at[
            : (section + 1) * width, section * width : (section + 1) * width
        ].set(first)
        blocks.append(current)
        full = current
    basis = jnp.concatenate(blocks, axis=1) * jnp.float32(N**0.5)
    return (basis, projection, first_pass)


def solution(mesh):
    return jax.shard_map(
        local,
        mesh=mesh,
        in_specs=(P("row", "col"), P()),
        out_specs=(P("row", None), P(), P()),
        check_vma=False,
    )
```

profile of v0, /device:TPU:1, one launch (start us, length us, event | category | flops | bytes accessed | tf_op | source)
XLA Modules:
  0.0 618.6 jit_solution(6120970448902567959)
XLA Ops:
  7.2 9.2 %copy.69 = f32[2048,1024]{0,1:T(8,128)} copy(f32[2048,1024]{1,0:T(8,128)} %param.17) | data formatting | bytes 16777216 | tf_op args[0]
  16.4 4.8 gather_fusion
  21.5 22.2 %all_to_all.57 = f32[16,128,128]{1,2,0:T(8,128)S(1)} all-to-all(f32[16,128,128]{1,2,0:T(8,128)S(1)} %fusion.2), channel_id=1, replica_groups=mesh['row'=8,'col'=16] {'col'}, dimensions={0} | all-to-all | bytes 2097152 | tf_op jit(solution)/shard_map/all_to_all | solution.py:22
  44.0 19.1 %all_to_all.58 = f32[16,128,128]{2,1,0:T(8,128)S(1)} all-to-all(f32[16,128,128]{2,1,0:T(8,128)S(1)} %broadcast_in_dim.55), channel_id=1, replica_groups=mesh['row'=8,'col'=16] {'col'}, dimensions={0} | all-to-all | bytes 2097152 | tf_op jit(solution)/shard_map/all_to_all | solution.py:41
  63.1 1.8 convolution_bitcast_fusion.8
  64.9 16.4 %all_to_all.59 = f32[8,128,128]{2,1,0:T(8,128)S(1)} all-to-all(f32[8,128,128]{2,1,0:T(8,128)S(1)} %broadcast_in_dim.56), channel_id=1, replica_groups=mesh['row'=8,'col'=16] {'row'}, dimensions={0} | all-to-all | bytes 1048576 | tf_op jit(solution)/shard_map/all_to_all | solution.py:41
  81.5 11.7 %cholesky.59 = f32[128,128]{1,0:T(8,128)S(1)} custom-call(f32[128,128]{1,0:T(8,128)S(1)} %fusion.16), custom_call_target="Cholesky" | custom-call | tf_op jit(solution)/shard_map/jit(cholesky)/cholesky | solution.py:72
  94.6 9.8 %custom-call.7 = f32[1,128,128]{1,2,0:T(8,128)S(1)} custom-call(f32[1,128,128]{2,1,0:T(8,128)S(1)} %fusion.9), custom_call_target="InvertDiagBlocksLowerTriangular" | custom-call | tf_op jit(solution)/shard_map/jit(_solve_triangular)/triangular_solve | solution.py:73
  104.4 2.0 fusion.14
  106.7 105.8 %all-gather.5.cloned.1.call-done = f32[16384,128]{0,1:T(8,128)} async-done(((f32[2048,128]{0,1:T(8,128)}), f32[16384,128]{0,1:T(8,128)}) %all-gather.5.cloned.1.call-update) | async-done | bytes 8388624 | tf_op jit(solution)/shard_map/all_gather | solution.py:11
  212.5 10.1 %copy.109 = f32[16,8,8,2048]{3,2,1,0:T(8,128)S(1)} copy(f32[16,8,8,2048]{3,1,2,0:T(8,128)} %bitcast.145) | data formatting | bytes 16777216
  222.6 1.2 constant_dynamic-slice_fusion.1
  223.8 8.9 %convolution_bitcast_fusion.7 = f32[16,16,8,128]{3,2,1,0:T(8,128)S(1)} fusion(f32[2048,1024]{1,0:T(8,128)S(1)} %bitcast.135, f32[1,1024,128]{1,0,2:T(1,128)S(1)} %constant_dynamic-slice_fusion.1), kind=kOutput, calls=%fused_computation.16 | convolution fusion | flops 3221225472 | bytes 9961472 | tf_op jit(solution)/shard_map/dot_general | solution.py:68
  232.8 20.8 %all_to_all.60 = f32[16,128,128]{1,2,0:T(8,128)S(1)} all-to-all(f32[16,128,128]{1,2,0:T(8,128)S(1)} %bitcast.147), channel_id=1, replica_groups=mesh['row'=8,'col'=16] {'col'}, dimensions={0} | all-to-all | bytes 2097152 | tf_op jit(solution)/shard_map/all_to_all | solution.py:22
  253.9 19.1 %all_to_all.61 = f32[16,128,128]{2,1,0:T(8,128)S(1)} all-to-all(f32[16,128,128]{2,1,0:T(8,128)S(1)} %broadcast_in_dim.57), channel_id=1, replica_groups=mesh['row'=8,'col'=16] {'col'}, dimensions={0} | all-to-all | bytes 2097152 | tf_op jit(solution)/shard_map/all_to_all | solution.py:41
  274.1 13.2 %all_to_all.62 = f32[8,128,128]{2,1,0:T(8,128)S(1)} all-to-all(f32[8,128,128]{2,1,0:T(8,128)S(1)} %broadcast_in_dim.58), channel_id=1, replica_groups=mesh['row'=8,'col'=16] {'row'}, dimensions={0} | all-to-all | bytes 1048576 | tf_op jit(solution)/shard_map/all_to_all | solution.py:41
  287.3 1.8 convolution_subtract_fusion.3
  289.1 1.8 convolution_bitcast_fusion.4
  291.0 1.1 convolution_bitcast_fusion.5
  292.7 16.6 %all_to_all.63 = f32[8,1,32768]{2,1,0:T(1,128)S(1)} all-to-all(f32[8,1,32768]{2,1,0:T(1,128)S(1)} %broadcast_in_dim.59), channel_id=1, replica_groups=mesh['row'=8,'col'=16] {'row'}, dimensions={0} | all-to-all | bytes 2097152 | tf_op jit(solution)/shard_map/all_to_all | solution.py:41
  310.1 1.8 fusion.1
  312.4 11.7 %cholesky.70 = f32[128,128]{1,0:T(8,128)S(1)} custom-call(f32[128,128]{1,0:T(8,128)S(1)} %fusion.13), custom_call_target="Cholesky" | custom-call | tf_op jit(solution)/shard_map/jit(cholesky)/cholesky | solution.py:72
  325.5 9.8 %custom-call.8 = f32[1,128,128]{1,2,0:T(8,128)S(1)} custom-call(f32[1,128,128]{2,1,0:T(8,128)S(1)} %get-tuple-element.99), custom_call_target="InvertDiagBlocksLowerTriangular" | custom-call | tf_op jit(solution)/shard_map/jit(_solve_triangular)/triangular_solve | solution.py:73
  335.3 2.0 convolution_bitcast_fusion.2
  337.4 108.9 %all-gather.7.cloned.1.call-done = f32[16384,128]{0,1:T(8,128)} async-done(((f32[2048,128]{0,1:T(8,128)}), f32[16384,128]{0,1:T(8,128)}) %all-gather.7.cloned.1.call-update) | async-done | bytes 8388624 | tf_op jit(solution)/shard_map/all_gather | solution.py:11
  446.2 10.2 %copy.110 = f32[16,8,8,2048]{3,2,1,0:T(8,128)S(1)} copy(f32[16,8,8,2048]{3,1,2,0:T(8,128)} %bitcast.146) | data formatting | bytes 16777216
  456.5 1.2 constant_dynamic-slice_fusion
  457.7 9.0 %convolution_bitcast_fusion.6 = f32[16,16,8,128]{3,2,1,0:T(8,128)S(1)} fusion(f32[2048,1024]{1,0:T(8,128)S(1)} %bitcast.137, f32[1,1024,128]{1,0,2:T(1,128)S(1)} %constant_dynamic-slice_fusion), kind=kOutput, calls=%fused_computation.15 | convolution fusion | flops 3221225472 | bytes 9961472 | tf_op jit(solution)/shard_map/dot_general | solution.py:68
  466.9 20.8 %all_to_all.64 = f32[16,128,128]{1,2,0:T(8,128)S(1)} all-to-all(f32[16,128,128]{1,2,0:T(8,128)S(1)} %bitcast.148), channel_id=1, replica_groups=mesh['row'=8,'col'=16] {'col'}, dimensions={0} | all-to-all | bytes 2097152 | tf_op jit(solution)/shard_map/all_to_all | solution.py:22
  488.0 19.1 %all_to_all.65 = f32[16,128,128]{2,1,0:T(8,128)S(1)} all-to-all(f32[16,128,128]{2,1,0:T(8,128)S(1)} %broadcast_in_dim.60), channel_id=1, replica_groups=mesh['row'=8,'col'=16] {'col'}, dimensions={0} | all-to-all | bytes 2097152 | tf_op jit(solution)/shard_map/all_to_all | solution.py:41
  508.0 1.8 fusion.3
  510.0 18.8 %all_to_all.66 = f32[8,256,128]{2,1,0:T(8,128)S(1)} all-to-all(f32[8,256,128]{2,1,0:T(8,128)S(1)} %broadcast_in_dim.61), channel_id=1, replica_groups=mesh['row'=8,'col'=16] {'row'}, dimensions={0} | all-to-all | bytes 2097152 | tf_op jit(solution)/shard_map/all_to_all | solution.py:41
  528.8 4.7 convolution_subtract_fusion.1
  533.5 1.8 convolution_bitcast_fusion.3
  535.3 1.8 convolution_bitcast_fusion
  537.1 2.0 broadcast_in_dim.62
  539.1 4.3 all-to-all-start.10
  547.1 17.4 %all-to-all-done.10 = f32[8,1,49152]{2,1,0:T(1,128)} async-done(((f32[8,1,49152]{2,1,0:T(1,128)}), f32[8,1,49152]{2,1,0:T(1,128)}, u32[]{:S(2)}, u32[]{:S(2)}) %all-to-all-start.10) | async-done | bytes 1572896 | tf_op jit(solution)/shard_map/all_to_all | solution.py:41
  564.5 2.6 reduce_sum.79
  567.0 4.4 fusion
  572.1 11.7 %cholesky.81 = f32[128,128]{1,0:T(8,128)S(1)} custom-call(f32[128,128]{1,0:T(8,128)S(1)} %fusion.11), custom_call_target="Cholesky" | custom-call | tf_op jit(solution)/shard_map/jit(cholesky)/cholesky | solution.py:72
  585.2 9.8 %custom-call.9 = f32[1,128,128]{1,2,0:T(8,128)S(1)} custom-call(f32[1,128,128]{2,1,0:T(8,128)S(1)} %get-tuple-element.97), custom_call_target="InvertDiagBlocksLowerTriangular" | custom-call | tf_op jit(solution)/shard_map/jit(_solve_triangular)/triangular_solve | solution.py:73
  595.1 2.3 convolution_bitcast_fusion.1
  597.4 2.0 maximum_multiply_fusion
  599.3 3.6 copy.91
  602.9 2.0 fusion.8
  604.9 2.8 scatter.24
  607.8 3.7 scatter.29
  (82 shorter events, 14.4 us)
Async XLA Ops:
  7.2 205.3 %all-gather.5.cloned.1.call-start = ((), (), s32[]{:S(2)}) async-start(), calls=%async_computation.11 | async-start | bytes 9437184 | tf_op jit(solution)/shard_map/all_gather | solution.py:11
  7.2 9.2 %copy-start.5 = (s32[128]{0:T(128)S(1)}, s32[128]{0:T(128)}, u32[]{:S(2)}) copy-start(s32[128]{0:T(128)} %param.18) | copy-start | bytes 1540
  106.4 339.8 %all-gather.7.cloned.1.call-start = ((), (), s32[]{:S(2)}) async-start(), calls=%async_computation.12 | async-start | bytes 9437184 | tf_op jit(solution)/shard_map/all_gather | solution.py:11
  212.5 11.3 %slice-start = ((s8[8388608]{0:T(1024)(128)(4,1)}), s8[4194304]{0:T(1024)(128)(4,1)S(1)}, s32[]{:S(2)}) async-start(s8[8388608]{0:T(1024)(128)(4,1)} %bitcast.134), calls=%async_computation.13 | async-start | bytes 8388608
  212.5 11.3 %slice-start.1 = ((s8[8388608]{0:T(1024)(128)(4,1)}), s8[4194304]{0:T(1024)(128)(4,1)S(1)}, s32[]{:S(2)}) async-start(s8[8388608]{0:T(1024)(128)(4,1)} %bitcast.134), calls=%async_computation.14 | async-start | bytes 8388608
  232.8 40.2 %copy-start = (f32[128,2048]{1,0:T(8,128)S(1)}, f32[128,2048]{1,0:T(8,128)}, u32[]{:S(2)}) copy-start(f32[128,2048]{1,0:T(8,128)} %fusion.14) | copy-start | bytes 3145732
  446.2 11.4 %slice-start.2 = ((s8[8388608]{0:T(1024)(128)(4,1)}), s8[4194304]{0:T(1024)(128)(4,1)S(1)}, s32[]{:S(2)}) async-start(s8[8388608]{0:T(1024)(128)(4,1)} %bitcast.136), calls=%async_computation.15 | async-start | bytes 8388608
  446.2 11.4 %slice-start.3 = ((s8[8388608]{0:T(1024)(128)(4,1)}), s8[4194304]{0:T(1024)(128)(4,1)S(1)}, s32[]{:S(2)}) async-start(s8[8388608]{0:T(1024)(128)(4,1)} %bitcast.136), calls=%async_computation.16 | async-start | bytes 8388608
  466.9 41.2 %copy-start.1 = (f32[2048,128]{0,1:T(8,128)S(1)}, f32[2048,128]{0,1:T(8,128)}, u32[]{:S(2)}) copy-start(f32[2048,128]{0,1:T(8,128)} %convolution_bitcast_fusion.2) | copy-start | bytes 3145732
  507.1 1.0 copy-start.2
  539.1 25.4 %all-to-all-start.10 = ((f32[8,1,49152]{2,1,0:T(1,128)}), f32[8,1,49152]{2,1,0:T(1,128)}, u32[]{:S(2)}, u32[]{:S(2)}) async-start(f32[8,1,49152]{2,1,0:T(1,128)} %broadcast_in_dim.62), calls=%async_computation.10 | async-start | bytes 3145728 | tf_op jit(solution)/shard_map/all_to_all | solution.py:41
  599.3 3.6 copy-start.3
  607.8 3.7 copy-start.4
Sparse Core Ops, SparseCore 0:
  106.6 105.8 all-gather.4
  337.5 108.7 all-gather.6
where the time goes:
time: 630 us; the launch traced here: 619 us
  waiting for transfers between devices  232 us (37%)
  blocking collectives  186 us (30%)
  other arithmetic  77.5 us (12%)
  local copies, waits for them, and re-layouts  54.5 us (9%)
  matrix products  49 us (8%)
  between operations  14.8 us (2%)
    all_gather x2, waiting for transfers between devices, picked_2(): lax.all_gather(value, axis)  215 us
    all_to_all x7, blocking collectives, copy_for_each(): return lax.all_to_all(copies, axis, split_axis=0, concat_axis=0, tiled=True)  122 us
    all_to_all x3, blocking collectives, sent_and_summed(): lax.all_to_all(cut_along(value, dim, devices), axis, 0, 0, tiled=True)  63.9 us
    dot_general x15, matrix products, product(): jnp.dot(left, right, precision=lax.Precision.HIGHEST, preferred_element_t...  42.6 us
    another operation x9, other arithmetic, finish_block(): lower = jnp.linalg.cholesky(gram)  37.2 us
    unnamed x24, local copies, waits for them, and re-layouts  34.1 us
    another operation x4, other arithmetic, finish_block(): jax.scipy.linalg.solve_triangular(lower, block.T, lower=True)  30.1 us
    all_to_all x1, waiting for transfers between devices, copy_for_each(): return lax.all_to_all(copies, axis, split_axis=0, concat_axis=0, tiled=True)  17.4 us
  transfers between devices with their start and end apart: 3, of which 3 were waited for; matrix products, arithmetic and copies ran while one was open for 1% of the time, Pallas kernels for 0%

commit v1 on v0

v1 whole, which is shorter than its diff:
```python
import jax
import jax.numpy as jnp
from jax import lax
from jax.experimental import pallas as pl
from jax.experimental.pallas import tpu as pltpu
from jax.sharding import PartitionSpec as P

N = 16384
B = 128
ITERS = 2
ROWS = 2048
COLS = 1024
NB = 16
MESH = pl.DeviceIdType.MESH
F32 = jnp.float32
BF16 = jnp.bfloat16
NN = (((1,), (0,)), ((), ()))
NT = (((1,), (1,)), ((), ()))
TN = (((0,), (0,)), ((), ()))


def exact(a, b, dims=NN):
    return lax.dot_general(a, b, dims, precision=lax.Precision.HIGHEST, preferred_element_type=F32)


def halves(a):
    high = a.astype(BF16)
    return high, (a - high.astype(F32)).astype(BF16)


def fine(a, b, dims=NN):
    ah, al = halves(a)
    bh, bl = halves(b)

    def dot(x, y):
        return lax.dot_general(x, y, dims, preferred_element_type=F32)

    return dot(ah, bh) + (dot(ah, bl) + dot(al, bh))


def factor(gram, aug, low):
    rows = lax.broadcasted_iota(jnp.int32, (B, B), 0)
    lanes = lax.broadcasted_iota(jnp.int32, (B, B), 1)
    aug[:, :B] = gram
    aug[:, B:] = jnp.where(rows == lanes, 1.0, 0.0).astype(F32)
    lane = lax.broadcasted_iota(jnp.int32, (NB, B), 1)
    sub = lax.broadcasted_iota(jnp.int32, (NB, B), 0)

    def panel(p, carry):
        o = pl.multiple_of(p * NB, NB)
        left = aug[pl.ds(o, NB), :B]
        right = aug[pl.ds(o, NB), B:]
        cols = []
        for t in range(NB):
            one = jnp.sum(jnp.where(lane == o + t, left, 0.0), axis=1, keepdims=True)
            cols.append(jnp.broadcast_to(one, (NB, B)))
        for t in range(NB):
            inv = lax.rsqrt(cols[t][t : t + 1, :])
            scale = jnp.where(sub == t, inv, 1.0)
            ratio = jnp.where(sub > t, cols[t] * inv, 0.0)
            left = left * scale
            right = right * scale
            left = left - ratio * left[t : t + 1, :]
            right = right - ratio * right[t : t + 1, :]
            for u in range(t + 1, NB):
                cols[u] = cols[u] - ratio * (cols[u][t : t + 1, :] * inv)
        left = jnp.where(lane >= o, left, 0.0)
        low[pl.ds(o, NB), :B] = jnp.where(lane >= o + sub, left, 0.0)
        low[pl.ds(o, NB), B:] = right
        both = jnp.concatenate([left, right], axis=1)
        aug[...] = aug[...] - exact(left, both, TN)
        return carry

    lax.fori_loop(0, B // NB, panel, 0)


def kernel(
    seed, cov, basis, projection, first_pass,
    cvm, chi, clo, stp, rs1, shard, vcol, srow, ypart, d2d, yown, rs2, yrow, q0, w1, wt, y1p, rs3, zrow, q1,
    scat, aug, low0, low1, low2, part, ga, gb, ha, hb, ia, ib, ja, jb, ka, kb,
    csem, rs1_s, rs1_r, ag1_s, ag1_r, tg1_s, tg1_r, d2d_s, d2d_r, rs2_s, rs2_r, ag2_s, ag2_r, fw_s, rs3_s, rs3_r, tg2_s, tg2_r,
    sa_s, sa_r, sb_s, sb_r,
):
    r = lax.axis_index("row")
    c = lax.axis_index("col")
    core = lax.rem(c, 2)
    chip = lax.div(c, 2)
    partner = c + 1 - 2 * core

    def loop(lo, hi, body):
        def run(i, carry):
            body(i)
            return carry

        lax.fori_loop(lo, hi, run, 0)

    def remote(src, dst, ssem, rsem, dev):
        return pltpu.make_async_remote_copy(src, dst, ssem, rsem, device_id=dev, device_id_type=MESH)

    def row_peer(k):
        return lax.rem(r + k, 8)

    def load(i):
        return pltpu.make_async_copy(cov.at[pl.ds(i * 256, 256)], cvm.at[pl.ds(i * 256, 256)], csem.at[i])

    loop(0, 8, lambda i: load(i).start())
    loop(0, 8, lambda i: load(i).wait())

    def gather(i):
        lines = []
        for t in range(8):
            at = seed[i * 8 + t] - r * ROWS
            inside = (at >= 0) & (at < ROWS)
            line = cvm[pl.ds(jnp.clip(at, 0, ROWS - 1), 1), :]
            lines.append(jnp.where(inside, line, 0.0))
        block = jnp.concatenate(lines, axis=0)
        for b in range(8):
            stp[b, pl.ds(pl.multiple_of(i * 8, 8), 8), :] = block[:, b * B : (b + 1) * B]

    loop(0, B // 8, gather)

    def row_scatter(src, dst, ssem, rsem):
        def send(k):
            to = row_peer(k)
            remote(src.at[to], dst.at[r], ssem.at[k], rsem.at[r], (to, c)).start()

        loop(1, 8, send)

    def row_scatter_sum(src, dst, ssem, rsem):
        def wait(k):
            src_row = row_peer(k)
            remote(src.at[0], dst.at[src_row], ssem.at[k], rsem.at[src_row], (r, c)).wait_recv()

        loop(1, 8, wait)
        dst[r] = src[r]
        total = dst[0]
        for i in range(1, 8):
            total = total + dst[i]
        return total

    row_scatter(stp, rs1, rs1_s, rs1_r)

    def split(i):
        blk = cvm[pl.ds(pl.multiple_of(i * B, B), B), :]
        high, rest = halves(blk)
        chi[lax.div(i, 2), lax.rem(i, 2)] = high
        clo[lax.div(i, 2), lax.rem(i, 2)] = rest

    loop(0, 16, split)

    start = row_scatter_sum(stp, rs1, rs1_s, rs1_r).T
    shard[0] = start
    vcol[r] = start

    def ag1(k):
        return remote(shard.at[0], vcol.at[r], ag1_s.at[k], ag1_r.at[r], (row_peer(k), c))

    loop(1, 8, lambda k: ag1(k).start())

    slot = core * 8 + r

    def place(src, dst, ssem, rsem):
        def send(k):
            to = lax.rem(c + k, 16)

            @pl.when(jnp.logical_or(chip != r, to != c))
            def _():
                remote(src, dst.at[slot], ssem.at[k], rsem.at[slot], (chip, to)).start()

        loop(0, 16, send)

    def placed(src, dst, ssem, rsem):
        def wait(s):
            mine = jnp.logical_and(lax.rem(s, 8) == r, 2 * r + lax.div(s, 8) == c)

            @pl.when(jnp.logical_not(mine))
            def _():
                remote(src, dst.at[s], ssem.at[0], rsem.at[s], (r, c)).wait_recv()

        loop(0, 16, wait)

        @pl.when(chip == r)
        def _():
            dst[slot] = src[...]

    def place_sent(src, dst, ssem, rsem):
        def wait(k):
            to = lax.rem(c + k, 16)

            @pl.when(jnp.logical_or(chip != r, to != c))
            def _():
                remote(src, dst.at[slot], ssem.at[k], rsem.at[slot], (chip, to)).wait_send()

        loop(0, 16, wait)

    place(shard.at[0], srow, tg1_s, tg1_r)

    def ag1_wait(k):
        src_row = row_peer(k)
        remote(shard.at[0], vcol.at[src_row], ag1_s.at[k], ag1_r.at[src_row], (r, c)).wait_recv()

    loop(1, 8, ag1_wait)

    def cat(i):
        high, rest = halves(vcol[i])
        scat[pl.ds(pl.multiple_of(i * B, B), B), :B] = high
        scat[pl.ds(pl.multiple_of(i * B, B), B), B:] = rest

    loop(0, 8, cat)

    def times(first, parity):
        a = chi[pl.ds(first, 4), parity].reshape(512, COLS)
        b = clo[pl.ds(first, 4), parity].reshape(512, COLS)
        full = jnp.dot(a, scat[...], preferred_element_type=F32) + jnp.dot(b, scat[...], preferred_element_type=F32)
        return (full[:, :B] + full[:, B:]).reshape(4, B, B)

    def across(h):
        return remote(ypart.at[pl.ds(h * 4, 4)], d2d.at[pl.ds(h * 4, 4)], d2d_s.at[h], d2d_r.at[h], (r, partner))

    def theirs(h):
        ypart[pl.ds(h * 4, 4)] = times(h * 4, 1 - core)
        across(h).start()

    loop(0, 2, theirs)

    def ours(h):
        yown[pl.ds(h * 4, 4)] = times(h * 4, core)

    loop(0, 2, ours)

    def rs2_send(i):
        return remote(yown.at[i], rs2.at[chip], rs2_s.at[i], rs2_r.at[chip], (r, 2 * i + core))

    def combine(h):
        across(h).wait_recv()
        for t in range(4):
            i = h * 4 + t
            yown[i] = yown[i] + d2d[i]

            @pl.when(i != chip)
            def _():
                rs2_send(i).start()

    loop(0, 2, combine)

    def small_start(src, buf, n, tag):
        buf[r] = src[pl.ds(pl.multiple_of(c * n, n), n), :]

        def send(k):
            remote(buf.at[r], buf.at[r], sa_s.at[tag, k], sa_r.at[tag, r], (row_peer(k), c)).start()

        loop(1, 8, send)

    def small_middle(buf, out, n, tag):
        def wait(k):
            src_row = row_peer(k)
            remote(buf.at[r], buf.at[src_row], sa_s.at[tag, k], sa_r.at[tag, src_row], (r, c)).wait_recv()

        loop(1, 8, wait)
        total = buf[0]
        for i in range(1, 8):
            total = total + buf[i]
        out[c] = total

        def send(k):
            to = lax.rem(c + k, 16)
            remote(out.at[c], out.at[c], sb_s.at[tag, k], sb_r.at[tag, c], (r, to)).start()

        loop(1, 16, send)

    def small_end(out, n, tag):
        def wait(k):
            src_col = lax.rem(c + k, 16)
            remote(out.at[c], out.at[src_col], sb_s.at[tag, k], sb_r.at[tag, src_col], (r, c)).wait_recv()

        loop(1, 16, wait)
        return out[...].reshape(16 * n, B)

    def small_sent(buf, out, tag):
        loop(1, 8, lambda k: remote(buf.at[r], buf.at[r], sa_s.at[tag, k], sa_r.at[tag, r], (r, c)).wait_send())
        loop(1, 16, lambda k: remote(out.at[c], out.at[c], sb_s.at[tag, k], sb_r.at[tag, c], (r, c)).wait_send())

    placed(shard.at[0], srow, tg1_s, tg1_r)
    part[0:B, :] = jnp.zeros((B, B), F32)

    def gram0(i):
        blk = srow[pl.ds(2 * i, 2)].reshape(256, B)
        part[0:B, :] += fine(blk, blk, TN)

    loop(0, 8, gram0)
    small_start(part, ga, 8, 0)

    def rs2_wait(i):
        @pl.when(i != chip)
        def _():
            remote(yown.at[i], rs2.at[i], rs2_s.at[i], rs2_r.at[i], (r, c)).wait_recv()

    loop(0, 8, rs2_wait)
    rs2[chip] = yown[chip]
    total = rs2[0]
    for i in range(1, 8):
        total = total + rs2[i]
    yrow[c] = total

    def ag2(i):
        return remote(yrow.at[c], yrow.at[c], ag2_s.at[i], ag2_r.at[c], (r, 2 * i + core))

    def ag2_send(i):
        @pl.when(i != chip)
        def _():
            ag2(i).start()

    loop(0, 8, ag2_send)
    to_partner = remote(yrow.at[c], yrow.at[c], fw_s.at[chip], ag2_r.at[c], (r, partner))
    to_partner.start()
    small_middle(ga, gb, 8, 0)

    def forward(i):
        return remote(yrow.at[2 * i + core], yrow.at[2 * i + core], fw_s.at[i], ag2_r.at[2 * i + core], (r, partner))

    def relay(k):
        i = lax.rem(chip + k, 8)
        remote(yrow.at[c], yrow.at[2 * i + core], ag2_s.at[i], ag2_r.at[2 * i + core], (r, c)).wait_recv()
        forward(i).start()

    loop(1, 8, relay)
    gram = small_end(gb, 8, 0)
    factor(gram, aug, low0)
    inv0 = low0[:, B:]

    def first_q(i):
        v = fine(srow[i], inv0, NT)
        q0[i] = v
        basis[pl.ds(pl.multiple_of(i * B, B), B), 0:B] = v * F32(N**0.5)

    loop(0, 16, first_q)

    def relayed(i):
        s = 2 * i + 1 - core
        remote(yrow.at[c], yrow.at[s], fw_s.at[i], ag2_r.at[s], (r, c)).wait_recv()

    loop(0, 8, relayed)

    part[0:B, :] = jnp.zeros((B, B), F32)

    def first_h(i):
        v = fine(yrow[i], inv0, NT)
        zrow[i] = v
        part[0:B, :] += fine(q0[i], v, TN)

    loop(0, 16, first_h)
    small_start(part, ha, 8, 1)
    small_middle(ha, hb, 8, 1)
    h1 = small_end(hb, 8, 1)
    first_pass[...] = jnp.zeros((3 * B, 2 * B), F32)
    projection[...] = jnp.zeros((3 * B, 2 * B), F32)
    first_pass[0:B, 0:B] = h1

    part[0 : 2 * B, :] = jnp.zeros((2 * B, B), F32)

    def once(i):
        w = zrow[i] - fine(q0[i], h1)
        w1[i] = w
        high, rest = halves(w.T)
        o = pl.multiple_of(i * B, B)
        wt[0:B, pl.ds(o, B)] = high
        wt[B : 2 * B, pl.ds(o, B)] = rest

    loop(0, 16, once)

    def times_t(k):
        q = lax.rem(lax.div(r, 2) + 1 + k, 4)
        o = pl.multiple_of(q * 256, 256)
        a = chi[:, :, :, pl.ds(o, 256)].reshape(ROWS, 256)
        b = clo[:, :, :, pl.ds(o, 256)].reshape(ROWS, 256)
        full = jnp.dot(wt[...], a, preferred_element_type=F32) + jnp.dot(wt[...], b, preferred_element_type=F32)
        half = full[:B, :] + full[B:, :]
        y1p[2 * q] = half[:, :B]
        y1p[2 * q + 1] = half[:, B:]
        for t in range(2):
            to = 2 * q + t

            @pl.when(to != r)
            def _():
                remote(y1p.at[to], rs3.at[r], rs3_s.at[to], rs3_r.at[r], (to, c)).start()

    loop(0, 4, times_t)

    def second_part(i):
        w = w1[i]
        part[0:B, :] += fine(q0[i], w, TN)
        part[B : 2 * B, :] += fine(w, w, TN)

    loop(0, 16, second_part)
    small_start(part, ia, 16, 2)

    def rs3_wait(i):
        @pl.when(i != r)
        def _():
            remote(y1p.at[i], rs3.at[i], rs3_s.at[i], rs3_r.at[i], (r, c)).wait_recv()

    loop(0, 8, rs3_wait)
    rs3[r] = y1p[r]
    total = rs3[0]
    for i in range(1, 8):
        total = total + rs3[i]
    shard[1] = total.T
    place(shard.at[1], q1, tg2_s, tg2_r)

    small_middle(ia, ib, 16, 2)
    sums = small_end(ib, 16, 2)
    h2 = sums[0:B, :]
    projection[0:B, 0:B] = h1 + h2
    factor(sums[B : 2 * B, :] - exact(h2, h2, TN), aug, low1)
    projection[B : 2 * B, 0:B] = low1[:, :B]
    inv1 = low1[:, B:]

    def second_q(i):
        v = fine(w1[i] - fine(q0[i], h2), inv1, NT)
        w1[i] = v
        basis[pl.ds(pl.multiple_of(i * B, B), B), B : 2 * B] = v * F32(N**0.5)

    loop(0, 16, second_q)
    placed(shard.at[1], q1, tg2_s, tg2_r)

    part[0 : 2 * B, :] = jnp.zeros((2 * B, B), F32)

    def image1(i):
        v = fine(q1[i] - fine(zrow[i], h2), inv1, NT)
        zrow[i] = v
        part[0:B, :] += fine(q0[i], v, TN)
        part[B : 2 * B, :] += fine(w1[i], v, TN)

    loop(0, 16, image1)
    small_start(part, ja, 16, 3)
    small_middle(ja, jb, 16, 3)
    h1b = small_end(jb, 16, 3)
    first_pass[0 : 2 * B, B : 2 * B] = h1b
    part[...] = jnp.zeros((3 * B, B), F32)

    def once1(i):
        w = zrow[i] - (fine(q0[i], h1b[0:B]) + fine(w1[i], h1b[B : 2 * B]))
        zrow[i] = w
        part[0:B, :] += fine(q0[i], w, TN)
        part[B : 2 * B, :] += fine(w1[i], w, TN)
        part[2 * B : 3 * B, :] += fine(w, w, TN)

    loop(0, 16, once1)
    small_start(part, ka, 24, 4)
    small_middle(ka, kb, 24, 4)
    sums1 = small_end(kb, 24, 4)
    h2b = sums1[0 : 2 * B, :]
    projection[0 : 2 * B, B : 2 * B] = h1b + h2b
    factor(sums1[2 * B : 3 * B, :] - exact(h2b, h2b, TN), aug, low2)
    projection[2 * B : 3 * B, B : 2 * B] = low2[:, :B]
    inv2 = low2[:, B:]

    def third_q(i):
        w = zrow[i] - (fine(q0[i], h2b[0:B]) + fine(w1[i], h2b[B : 2 * B]))
        basis[pl.ds(pl.multiple_of(i * B, B), B), 2 * B : 3 * B] = fine(w, inv2, NT) * F32(N**0.5)

    loop(0, 16, third_q)

    loop(1, 8, lambda k: remote(stp.at[0], rs1.at[r], rs1_s.at[k], rs1_r.at[r], (r, c)).wait_send())
    loop(1, 8, lambda k: ag1(k).wait_send())
    place_sent(shard.at[0], srow, tg1_s, tg1_r)
    loop(0, 2, lambda h: across(h).wait_send())

    def sent(i):
        @pl.when(i != chip)
        def _():
            rs2_send(i).wait_send()
            ag2(i).wait_send()

        forward(i).wait_send()

        @pl.when(i != r)
        def _():
            remote(y1p.at[i], rs3.at[r], rs3_s.at[i], rs3_r.at[r], (r, c)).wait_send()

    loop(0, 8, sent)
    place_sent(shard.at[1], q1, tg2_s, tg2_r)
    for tag, (a, b) in enumerate(((ga, gb), (ha, hb), (ia, ib), (ja, jb), (ka, kb))):
        small_sent(a, b, tag)


def local(covariance, seed_index):
    v = pltpu.VMEM
    dma = pltpu.SemaphoreType.DMA
    blocks8 = v((8, B, B), F32)
    blocks16 = v((16, B, B), F32)
    small = []
    for n in (8, 8, 16, 16, 24):
        small += [v((8, n, B), F32), v((16, n, B), F32)]
    scratch = [
        v((ROWS, COLS), F32), v((8, 2, B, COLS), BF16), v((8, 2, B, COLS), BF16),
        blocks8, blocks8, v((2, B, B), F32), blocks8, blocks16,
        blocks8, blocks8, blocks8, blocks8, blocks16,
        blocks16, blocks16, v((2 * B, ROWS), BF16), blocks8, blocks8, blocks16, blocks16,
        v((COLS, 2 * B), BF16), v((B, 2 * B), F32), v((B, 2 * B), F32), v((B, 2 * B), F32), v((B, 2 * B), F32),
        v((3 * B, B), F32), *small,
        dma((8,)), dma((8,)), dma((8,)), dma((8,)), dma((8,)), dma((16,)), dma((16,)),
        dma((2,)), dma((2,)), dma((8,)), dma((8,)), dma((8,)), dma((16,)), dma((8,)), dma((8,)), dma((8,)),
        dma((16,)), dma((16,)),
        dma((5, 8)), dma((5, 8)), dma((5, 16)), dma((5, 16)),
    ]
    basis, projection, first_pass = pl.pallas_call(
        kernel,
        out_shape=(
            jax.ShapeDtypeStruct((ROWS, 3 * B), F32),
            jax.ShapeDtypeStruct((3 * B, 2 * B), F32),
            jax.ShapeDtypeStruct((3 * B, 2 * B), F32),
        ),
        in_specs=[pl.BlockSpec(memory_space=pltpu.SMEM), pl.BlockSpec(memory_space=pl.ANY)],
        out_specs=[pl.BlockSpec(memory_space=pltpu.VMEM)] * 3,
        scratch_shapes=scratch,
        compiler_params=pltpu.CompilerParams(has_side_effects=True, vmem_limit_bytes=60 * 2**20),
        name="lanczos",
    )(seed_index, covariance)
    return basis, projection, first_pass


def solution(mesh):
    return jax.shard_map(
        local,
        mesh=mesh,
        in_specs=(P("row", "col"), P()),
        out_specs=(P("row", None), P(), P()),
        check_vma=False,
    )
```

time: 630 us -> 252 us (0.40); the launches traced: 619 us -> 252 us
  Pallas kernels: 0 us -> 246 us
  waiting for transfers between devices: 232 us -> 0 us
  blocking collectives: 186 us -> 0 us
  other arithmetic: 77.5 us -> 0 us
  local copies, waits for them, and re-layouts: 54.5 us -> 5.33 us
  matrix products: 49 us -> 0 us
  between operations: 14.8 us -> 0.66 us
    pallas_call x0 -> x1, Pallas kernels: none -> 246 us  [local(): pl.pallas_call(kernel, out_shape=(jax.ShapeDtypeStruct((ROWS, 3 * B), F32...]
    all_gather x2 -> x0, waiting for transfers between devices: 215 us -> none  [picked_2(): lax.all_gather(value, axis)]
    all_to_all x10 -> x0, blocking collectives: 186 us -> none  [the longest x7 122 us: copy_for_each(): return lax.all_to_all(copies, axis, split_axis=0, concat_axis=0, tiled=True)]
    another operation x18 -> x0, other arithmetic: 71.6 us -> none  [the longest x9 37.2 us: finish_block(): lower = jnp.linalg.cholesky(gram)]
    dot_general x15 -> x0, matrix products: 42.6 us -> none  [product(): jnp.dot(left, right, precision=lax.Precision.HIGHEST, preferred_element_t...]
    unnamed x24 -> x7, local copies, waits for them, and re-layouts: 34.1 us -> 5.33 us
    all_to_all x1 -> x0, waiting for transfers between devices: 17.4 us -> none  [copy_for_each(): return lax.all_to_all(copies, axis, split_axis=0, concat_axis=0, tiled=True)]
    scatter x6 -> x0, local copies, waits for them, and re-layouts: 8.66 us -> none  [the longest x2 4.48 us: local(): first_pass = first_pass.at[:(section + 1) * width, section * width:(secti...]
  transfers between devices with their start and end apart: 3 -> 0, of which waited for: 3 -> 0; matrix products, arithmetic and copies ran while one was open for 1% -> 0% of each run, Pallas kernels for 0% -> 0%
where the time goes in v1:
time: 252 us
  Pallas kernels  246 us (98%)
  local copies, waits for them, and re-layouts  5.33 us (2%)
    pallas_call x1, Pallas kernels, local(): pl.pallas_call(kernel, out_shape=(jax.ShapeDtypeStruct((ROWS, 3 * B), F32...  246 us
    unnamed x7, local copies, waits for them, and re-layouts  5.33 us

profile of v1, /device:TPU:1, one launch (start us, length us, event | category | flops | bytes accessed | tf_op | source)
XLA Modules:
  0.0 252.1 jit_solution(5425394959634901100)
XLA Ops:
  0.6 246.2 %lanczos.1 = (f32[2048,384]{1,0:T(8,128)}, f32[384,256]{1,0:T(8,128)}, f32[384,256]{1,0:T(8,128)}) custom-call(s32[128]{0:T(128)} %seed.1, f32[2048,1024]{1,0:T(8,128)} %cov.1), custom_call_target="tpu_custom_call" | custom-call | tf_op jit(solution)/shard_map/lanczos/pallas_call | solution.py:507
  246.8 0.0 copy-start.1
  246.8 0.0 copy-start
  246.8 3.8 %copy.8 = f32[2048,384]{1,0:T(8,128)} copy(f32[2048,384]{1,0:T(8,128)} %get-tuple-element.6) | data formatting | bytes 6291456
  250.6 0.0 copy-done.1
  250.6 0.7 copy.9
  251.4 0.0 copy-done
  251.4 0.7 copy.10
Async XLA Ops:
  246.8 3.8 %copy-start.1 = (f32[384,256]{1,0:T(8,128)S(1)}, f32[384,256]{1,0:T(8,128)}, u32[]{:S(2)}) copy-start(f32[384,256]{1,0:T(8,128)} %get-tuple-element.7) | copy-start | bytes 1179652
  246.8 4.6 %copy-start = (f32[384,256]{1,0:T(8,128)S(1)}, f32[384,256]{1,0:T(8,128)}, u32[]{:S(2)}) copy-start(f32[384,256]{1,0:T(8,128)} %get-tuple-element.8) | copy-start | bytes 1179652

commit v2 on v1

v2 whole, which is shorter than its diff:
```python
import jax
import jax.numpy as jnp
from jax import lax
from jax.experimental import pallas as pl
from jax.experimental.pallas import tpu as pltpu
from jax.sharding import PartitionSpec as P

N = 16384
B = 128
ITERS = 2
ROWS = 2048
COLS = 1024
NB = 16
MESH = pl.DeviceIdType.MESH
F32 = jnp.float32
BF16 = jnp.bfloat16
NN = (((1,), (0,)), ((), ()))
NT = (((1,), (1,)), ((), ()))
TN = (((0,), (0,)), ((), ()))


def exact(a, b, dims=NN):
    return lax.dot_general(a, b, dims, precision=lax.Precision.HIGHEST, preferred_element_type=F32)


def halves(a):
    high = a.astype(BF16)
    return high, (a - high.astype(F32)).astype(BF16)


def fine(a, b, dims=NN):
    ah, al = halves(a)
    bh, bl = halves(b)

    def dot(x, y):
        return lax.dot_general(x, y, dims, preferred_element_type=F32)

    both = dot(jnp.concatenate([ah, al], axis=0), bh)
    n = a.shape[0]
    return both[:n] + (both[n:] + dot(ah, bl))


def factor(gram, aug, low):
    rows = lax.broadcasted_iota(jnp.int32, (B, B), 0)
    lanes = lax.broadcasted_iota(jnp.int32, (B, B), 1)
    aug[:, :B] = gram
    aug[:, B:] = jnp.where(rows == lanes, 1.0, 0.0).astype(F32)
    lane = lax.broadcasted_iota(jnp.int32, (NB, B), 1)
    sub = lax.broadcasted_iota(jnp.int32, (NB, B), 0)

    def panel(p, carry):
        o = pl.multiple_of(p * NB, NB)
        left = aug[pl.ds(o, NB), :B]
        right = aug[pl.ds(o, NB), B:]
        cols = []
        for t in range(NB):
            one = jnp.sum(jnp.where(lane == o + t, left, 0.0), axis=1, keepdims=True)
            cols.append(jnp.broadcast_to(one, (NB, B)))
        for t in range(NB):
            inv = lax.rsqrt(cols[t][t : t + 1, :])
            scale = jnp.where(sub == t, inv, 1.0)
            ratio = jnp.where(sub > t, cols[t] * inv, 0.0)
            left = left * scale
            right = right * scale
            left = left - ratio * left[t : t + 1, :]
            right = right - ratio * right[t : t + 1, :]
            for u in range(t + 1, NB):
                cols[u] = cols[u] - ratio * (cols[u][t : t + 1, :] * inv)
        left = jnp.where(lane >= o, left, 0.0)
        low[pl.ds(o, NB), :B] = jnp.where(lane >= o + sub, left, 0.0)
        low[pl.ds(o, NB), B:] = right
        both = jnp.concatenate([left, right], axis=1)
        aug[...] = aug[...] - exact(left, both, TN)
        return carry

    lax.fori_loop(0, B // NB, panel, 0)


def kernel(
    seed, cov, p_out, l_out, h_out, f_out,
    cvm, chi, clo, stp, rs1, vcol, st, ypart, d2d, yown, rs2, yt, zt, pt, wt, y1p, rs3, tsh, last, projection, first_pass,
    scat, aug, low0, low1, low2, ga, gb, ha, hb, ia, ib, ja, jb, ka, kb,
    csem, osem, rs1_s, rs1_r, ag1_s, ag1_r, t_s, t_r, d2d_s, d2d_r, rs2_s, rs2_r, ag_s, ag_r, fw_s, rs3_s, rs3_r,
    sa_s, sa_r, sb_s, sb_r,
):
    r = lax.axis_index("row")
    c = lax.axis_index("col")
    core = lax.rem(c, 2)
    chip = lax.div(c, 2)
    partner = c + 1 - 2 * core
    there = (chip, core * 8 + r)
    origin = (lax.rem(c, 8), 2 * r + lax.div(c, 8))
    stays = jnp.logical_and(there[0] == r, there[1] == c)

    def loop(lo, hi, body):
        def run(i, carry):
            body(i)
            return carry

        lax.fori_loop(lo, hi, run, 0)

    def remote(src, dst, ssem, rsem, dev):
        return pltpu.make_async_remote_copy(src, dst, ssem, rsem, device_id=dev, device_id_type=MESH)

    def row_peer(k):
        return lax.rem(r + k, 8)

    def col_peer(k):
        return lax.rem(c + k, 16)

    def block(i):
        return pl.ds(pl.multiple_of(i * B, B), B)

    def load(i):
        return pltpu.make_async_copy(cov.at[pl.ds(i * 256, 256)], cvm.at[pl.ds(i * 256, 256)], csem.at[i])

    loop(0, 8, lambda i: load(i).start())
    barrier = pltpu.get_barrier_semaphore()

    def greet(dev):
        pl.semaphore_signal(barrier, inc=1, device_id=dev, device_id_type=MESH)

    loop(1, 8, lambda k: greet((row_peer(k), c)))
    loop(1, 16, lambda k: greet((r, col_peer(k))))

    @pl.when(jnp.logical_not(stays))
    def _():
        greet(there)
        greet(origin)

    loop(0, 8, lambda i: load(i).wait())

    def gather(i):
        lines = []
        for t in range(8):
            at = seed[i * 8 + t] - r * ROWS
            inside = (at >= 0) & (at < ROWS)
            line = cvm[pl.ds(jnp.clip(at, 0, ROWS - 1), 1), :]
            lines.append(jnp.where(inside, line, 0.0))
        full = jnp.concatenate(lines, axis=0)
        for b in range(8):
            stp[b, pl.ds(pl.multiple_of(i * 8, 8), 8), :] = full[:, b * B : (b + 1) * B]

    loop(0, B // 8, gather)

    @pl.when(stays)
    def _():
        pl.semaphore_wait(barrier, 22)

    @pl.when(jnp.logical_not(stays))
    def _():
        pl.semaphore_wait(barrier, 24)

    def rs1_send(k):
        to = row_peer(k)
        remote(stp.at[to], rs1.at[r], rs1_s.at[to], rs1_r.at[r], (to, c)).start()

    loop(1, 8, rs1_send)

    def split(i):
        high, rest = halves(cvm[block(i), :])
        chi[lax.div(i, 2), lax.rem(i, 2)] = high
        clo[lax.div(i, 2), lax.rem(i, 2)] = rest

    loop(0, 16, split)

    def row_sum(src, dst, ssem, rsem):
        def wait(i):
            @pl.when(i != r)
            def _():
                remote(src.at[i], dst.at[i], ssem.at[i], rsem.at[i], (r, c)).wait_recv()

        loop(0, 8, wait)
        dst[r] = src[r]
        total = dst[0]
        for i in range(1, 8):
            total = total + dst[i]
        return total

    start = row_sum(stp, rs1, rs1_s, rs1_r)
    vcol[:, block(r)] = start
    tsh[0] = start

    def ag1(k):
        return remote(vcol.at[:, block(r)], vcol.at[:, block(r)], ag1_s.at[k], ag1_r.at[r], (row_peer(k), c))

    loop(1, 8, lambda k: ag1(k).start())

    def turn(tag, dst):
        return remote(tsh.at[tag], dst.at[0:B, block(there[1])], t_s.at[tag], t_r.at[tag], there)

    def turn_start(tag, dst):
        @pl.when(jnp.logical_not(stays))
        def _():
            turn(tag, dst).start()

    def turn_wait(tag, dst):
        @pl.when(jnp.logical_not(stays))
        def _():
            remote(tsh.at[tag], dst.at[0:B, block(c)], t_s.at[tag], t_r.at[tag], there).wait_recv()

        @pl.when(stays)
        def _():
            dst[0:B, block(c)] = tsh[tag]

    turn_start(0, st)

    def ag1_wait(k):
        i = row_peer(k)
        remote(vcol.at[:, block(i)], vcol.at[:, block(i)], ag1_s.at[k], ag1_r.at[i], (r, c)).wait_recv()

    loop(1, 8, ag1_wait)

    def gather_start(buf, tag):
        mine = buf.at[0:B, block(c)]

        def send(k):
            i = lax.rem(chip + k, 8)
            remote(mine, mine, ag_s.at[tag, i], ag_r.at[tag, c], (r, 2 * i + core)).start()

        loop(1, 8, send)
        remote(mine, mine, fw_s.at[tag, chip], ag_r.at[tag, c], (r, partner)).start()

    def gather_relay(buf, tag):
        def relay(k):
            i = lax.rem(chip + 8 - k, 8)
            s = 2 * i + core
            got = buf.at[0:B, block(s)]
            remote(got, got, ag_s.at[tag, i], ag_r.at[tag, s], (r, c)).wait_recv()
            remote(got, got, fw_s.at[tag, i], ag_r.at[tag, s], (r, partner)).start()

        loop(1, 8, relay)

    def gather_wait(buf, tag):
        def wait(i):
            s = 2 * i + 1 - core
            got = buf.at[0:B, block(s)]
            remote(got, got, fw_s.at[tag, i], ag_r.at[tag, s], (r, c)).wait_recv()

        loop(0, 8, wait)

    def gather_sent(buf, tag):
        mine = buf.at[0:B, block(c)]

        def wait(i):
            @pl.when(i != chip)
            def _():
                remote(mine, mine, ag_s.at[tag, i], ag_r.at[tag, c], (r, c)).wait_send()

            remote(mine, mine, fw_s.at[tag, i], ag_r.at[tag, c], (r, c)).wait_send()

        loop(0, 8, wait)

    def spread(out, at, n_peers, ssem, rsem, tag, dev):
        loop(1, n_peers, lambda k: remote(out.at[at], out.at[at], ssem.at[tag, k], rsem.at[tag, at], dev(k)).start())

    def collect(out, at, n_peers, ssem, rsem, tag):
        def wait(k):
            i = lax.rem(at + k, n_peers)
            remote(out.at[i], out.at[i], ssem.at[tag, k], rsem.at[tag, i], (r, c)).wait_recv()

        loop(1, n_peers, wait)

    def spread_sent(out, at, n_peers, ssem, rsem, tag):
        loop(1, n_peers, lambda k: remote(out.at[at], out.at[at], ssem.at[tag, k], rsem.at[tag, at], (r, c)).wait_send())

    def over_row(k):
        return (row_peer(k), c)

    def over_col(k):
        return (r, col_peer(k))

    def added(buf, n):
        total = buf[0]
        for i in range(1, n):
            total = total + buf[i]
        return total

    ga[c] = fine(vcol[pl.ds(pl.multiple_of(r * 16, 16), 16), :], vcol[...], NT)
    spread(ga, c, 16, sb_s, sb_r, 0, over_col)

    def cat(i):
        high, rest = halves(vcol[:, block(i)].T)
        scat[block(i), :B] = high
        scat[block(i), B:] = rest

    loop(0, 8, cat)

    def times(first, parity):
        a = chi[pl.ds(first, 4), parity].reshape(512, COLS)
        b = clo[pl.ds(first, 4), parity].reshape(512, COLS)
        full = jnp.dot(a, scat[...], preferred_element_type=F32) + jnp.dot(b, scat[...], preferred_element_type=F32)
        return (full[:, :B] + full[:, B:]).reshape(4, B, B)

    def across(h):
        return remote(ypart.at[pl.ds(h * 4, 4)], d2d.at[pl.ds(h * 4, 4)], d2d_s.at[h], d2d_r.at[h], (r, partner))

    def theirs(h):
        ypart[pl.ds(h * 4, 4)] = times(h * 4, 1 - core)
        across(h).start()

    loop(0, 2, theirs)
    turn_wait(0, st)
    gather_start(st, 0)

    def ours(h):
        yown[pl.ds(h * 4, 4)] = times(h * 4, core)

    loop(0, 2, ours)

    def rs2_copy(i):
        return remote(yown.at[i], rs2.at[chip], rs2_s.at[i], rs2_r.at[chip], (r, 2 * i + core))

    def combine(h):
        across(h).wait_recv()
        for t in range(4):
            i = h * 4 + t
            yown[i] = yown[i] + d2d[i]

            @pl.when(i != chip)
            def _():
                rs2_copy(i).start()

    loop(0, 2, combine)

    collect(ga, c, 16, sb_s, sb_r, 0)
    gb[r] = added(ga, 16)
    spread(gb, r, 8, sa_s, sa_r, 0, over_row)
    gather_relay(st, 0)

    def rs2_wait(i):
        @pl.when(i != chip)
        def _():
            remote(yown.at[i], rs2.at[i], rs2_s.at[i], rs2_r.at[i], (r, c)).wait_recv()

    loop(0, 8, rs2_wait)
    rs2[chip] = yown[chip]
    yt[:, block(c)] = added(rs2, 8).T
    gather_start(yt, 1)

    collect(gb, r, 8, sa_s, sa_r, 0)
    factor(gb[...].reshape(B, B), aug, low0)
    inv0 = low0[:, B:]
    gather_wait(st, 0)

    def put(i):
        return pltpu.make_async_copy(pt.at[pl.ds(i * B, B)], p_out.at[pl.ds(i * B, B)], osem.at[i])

    def first_q(i):
        o = pl.ds(pl.multiple_of(i * 512, 512), 512)
        pt[0:B, o] = fine(inv0, st[:, o])

    loop(0, 4, first_q)
    put(0).start()
    gather_relay(yt, 1)
    gather_wait(yt, 1)

    def small_start(value, buf, tag):
        buf[r] = value
        spread(buf, r, 8, sa_s, sa_r, tag, over_row)

    def small_middle(buf, out, tag):
        collect(buf, r, 8, sa_s, sa_r, tag)
        out[c] = added(buf, 8)
        spread(out, c, 16, sb_s, sb_r, tag, over_col)

    def small_end(out, n, tag):
        collect(out, c, 16, sb_s, sb_r, tag)
        return out[...].reshape(16 * n, B)

    def share(n):
        return pl.ds(pl.multiple_of(c * n, 8), n)

    small_start(fine(pt[share(8), :], yt[...], NT), ha, 1)

    def first_image(i):
        o = pl.ds(pl.multiple_of(i * 512, 512), 512)
        zt[B : 2 * B, o] = fine(inv0, yt[:, o])

    loop(0, 4, first_image)
    first_pass[...] = jnp.zeros((3 * B, 2 * B), F32)
    projection[...] = jnp.zeros((3 * B, 2 * B), F32)
    small_middle(ha, hb, 1)
    h1 = exact(small_end(hb, 8, 1), inv0, NT)
    first_pass[0:B, 0:B] = h1
    h1t = h1.T

    def once(i):
        o = pl.ds(pl.multiple_of(i * 512, 512), 512)
        w = zt[B : 2 * B, o] - fine(h1t, pt[0:B, o])
        pt[B : 2 * B, o] = w
        high, rest = halves(w)
        wt[0:B, o] = high
        wt[B : 2 * B, o] = rest

    loop(0, 4, once)

    def times_t(k):
        q = lax.rem(lax.div(r, 2) + 1 + k, 4)
        o = pl.ds(pl.multiple_of(q * 256, 256), 256)
        a = chi[:, :, :, o].reshape(ROWS, 256)
        b = clo[:, :, :, o].reshape(ROWS, 256)
        full = jnp.dot(wt[...], a, preferred_element_type=F32) + jnp.dot(wt[...], b, preferred_element_type=F32)
        half = full[:B, :] + full[B:, :]
        y1p[2 * q] = half[:, :B]
        y1p[2 * q + 1] = half[:, B:]
        for t in range(2):
            to = 2 * q + t

            @pl.when(to != r)
            def _():
                remote(y1p.at[to], rs3.at[r], rs3_s.at[to], rs3_r.at[r], (to, c)).start()

    loop(0, 4, times_t)

    small_start(fine(pt[share(16), :], pt[B : 2 * B, :], NT), ia, 2)
    tsh[1] = row_sum(y1p, rs3, rs3_s, rs3_r)
    turn_start(1, zt)
    small_middle(ia, ib, 2)
    turn_wait(1, zt)
    gather_start(zt, 2)
    sums = small_end(ib, 16, 2)
    h2 = sums[0:B, :]
    h2t = h2.T
    projection[0:B, 0:B] = h1 + h2
    factor(sums[B : 2 * B, :] - exact(h2, h2, TN), aug, low1)
    projection[B : 2 * B, 0:B] = low1[:, :B]
    inv1 = low1[:, B:]
    gather_relay(zt, 2)

    def second_q(i):
        o = pl.ds(pl.multiple_of(i * 512, 512), 512)
        pt[B : 2 * B, o] = fine(inv1, pt[B : 2 * B, o] - fine(h2t, pt[0:B, o]))

    loop(0, 4, second_q)
    put(1).start()
    mix = jnp.concatenate([inv1, -exact(inv1, h2t)], axis=1)
    gather_wait(zt, 2)

    def image1(i):
        o = pl.ds(pl.multiple_of(i * 512, 512), 512)
        pt[2 * B : 3 * B, o] = fine(mix, zt[:, o])

    loop(0, 4, image1)
    small_start(fine(pt[share(16), :], pt[2 * B : 3 * B, :], NT), ja, 3)
    small_middle(ja, jb, 3)
    h1b = small_end(jb, 16, 3)
    first_pass[0 : 2 * B, B : 2 * B] = h1b
    passed = pltpu.make_async_copy(first_pass, f_out, osem.at[3])
    passed.start()
    h1bt = h1b.T

    def once1(i):
        o = pl.ds(pl.multiple_of(i * 512, 512), 512)
        pt[2 * B : 3 * B, o] = pt[2 * B : 3 * B, o] - fine(h1bt, pt[0 : 2 * B, o])

    loop(0, 4, once1)
    put(2).start()
    small_start(fine(pt[share(24), :], pt[2 * B : 3 * B, :], NT), ka, 4)
    small_middle(ka, kb, 4)
    sums1 = small_end(kb, 24, 4)
    h2b = sums1[0 : 2 * B, :]
    projection[0 : 2 * B, B : 2 * B] = h1b + h2b
    factor(sums1[2 * B : 3 * B, :] - exact(h2b, h2b, TN), aug, low2)
    projection[2 * B : 3 * B, B : 2 * B] = low2[:, :B]
    inv2 = low2[:, B:]
    projected = pltpu.make_async_copy(projection, h_out, osem.at[4])
    projected.start()
    last[...] = jnp.concatenate([-exact(inv2, h2b, NT), inv2], axis=1)
    mixed = pltpu.make_async_copy(last, l_out, osem.at[5])
    mixed.start()

    def sent(i):
        @pl.when(i != r)
        def _():
            remote(stp.at[i], rs1.at[r], rs1_s.at[i], rs1_r.at[r], (r, c)).wait_send()
            remote(y1p.at[i], rs3.at[r], rs3_s.at[i], rs3_r.at[r], (r, c)).wait_send()

        @pl.when(i != chip)
        def _():
            rs2_copy(i).wait_send()

    loop(0, 8, sent)
    loop(1, 8, lambda k: ag1(k).wait_send())

    @pl.when(jnp.logical_not(stays))
    def _():
        turn(0, st).wait_send()
        turn(1, zt).wait_send()

    loop(0, 2, lambda h: across(h).wait_send())
    for tag, buf in enumerate((st, yt, zt)):
        gather_sent(buf, tag)
    spread_sent(ga, c, 16, sb_s, sb_r, 0)
    spread_sent(gb, r, 8, sa_s, sa_r, 0)
    for tag, (a, b) in enumerate(((ha, hb), (ia, ib), (ja, jb), (ka, kb)), 1):
        spread_sent(a, r, 8, sa_s, sa_r, tag)
        spread_sent(b, c, 16, sb_s, sb_r, tag)
    for i in range(3):
        put(i).wait()
    passed.wait()
    projected.wait()
    mixed.wait()


def finish(p, l, h, f, basis, projection, first_pass):
    basis[:, : 2 * B] = p[: 2 * B, :].T * F32(N**0.5)
    basis[:, 2 * B :] = fine(l[...], p[...]).T * F32(N**0.5)
    projection[...] = h[...]
    first_pass[...] = f[...]


def local(covariance, seed_index):
    v = pltpu.VMEM
    dma = pltpu.SemaphoreType.DMA
    blocks8 = v((8, B, B), F32)
    wide = v((B, ROWS), F32)
    square = v((B, 2 * B), F32)
    small = [v((16, 16, B), F32), v((8, 16, B), F32)]
    for n in (8, 16, 16, 24):
        small += [v((8, n, B), F32), v((16, n, B), F32)]
    scratch = [
        v((ROWS, COLS), F32), v((8, 2, B, COLS), BF16), v((8, 2, B, COLS), BF16),
        blocks8, blocks8, v((B, COLS), F32), wide,
        blocks8, blocks8, blocks8, blocks8, wide,
        v((2 * B, ROWS), F32), v((3 * B, ROWS), F32), v((2 * B, ROWS), BF16), blocks8, blocks8, v((2, B, B), F32),
        v((B, 3 * B), F32), v((3 * B, 2 * B), F32), v((3 * B, 2 * B), F32),
        v((COLS, 2 * B), BF16), square, square, square, square, *small,
        dma((8,)), dma((6,)), dma((8,)), dma((8,)), dma((8,)), dma((8,)), dma((2,)), dma((2,)),
        dma((2,)), dma((2,)), dma((8,)), dma((8,)), dma((3, 8)), dma((3, 16)), dma((3, 8)), dma((8,)), dma((8,)),
        dma((5, 8)), dma((5, 8)), dma((5, 16)), dma((5, 16)),
    ]
    any_space = pl.BlockSpec(memory_space=pl.ANY)
    wide_p, mix, square_h, square_f = pl.pallas_call(
        kernel,
        out_shape=(
            jax.ShapeDtypeStruct((3 * B, ROWS), F32),
            jax.ShapeDtypeStruct((B, 3 * B), F32),
            jax.ShapeDtypeStruct((3 * B, 2 * B), F32),
            jax.ShapeDtypeStruct((3 * B, 2 * B), F32),
        ),
        in_specs=[pl.BlockSpec(memory_space=pltpu.SMEM), any_space],
        out_specs=[any_space] * 4,
        scratch_shapes=scratch,
        compiler_params=pltpu.CompilerParams(collective_id=0, has_side_effects=True, vmem_limit_bytes=60 * 2**20),
        name="lanczos",
    )(seed_index, covariance)
    whole = pl.BlockSpec((3 * B, 2 * B), lambda i: (0, 0))
    return pl.pallas_call(
        finish,
        grid=(4,),
        out_shape=(
            jax.ShapeDtypeStruct((ROWS, 3 * B), F32),
            jax.ShapeDtypeStruct((3 * B, 2 * B), F32),
            jax.ShapeDtypeStruct((3 * B, 2 * B), F32),
        ),
        in_specs=[pl.BlockSpec((3 * B, 512), lambda i: (0, i)), pl.BlockSpec((B, 3 * B), lambda i: (0, 0)), whole, whole],
        out_specs=(pl.BlockSpec((512, 3 * B), lambda i: (i, 0)), whole, whole),
        name="finish",
    )(wide_p, mix, square_h, square_f)


def solution(mesh):
    return jax.shard_map(
        local,
        mesh=mesh,
        in_specs=(P("row", "col"), P()),
        out_specs=(P("row", None), P(), P()),
        check_vma=False,
    )
```

time: 252 us -> 131 us (0.52)
  Pallas kernels: 246 us -> 130 us
  local copies, waits for them, and re-layouts: 5.33 us -> 0 us
    pallas_call x1 -> x2, Pallas kernels: 246 us -> 130 us  [the longest x1 124 us: local(): pl.pallas_call(kernel, out_shape=(jax.ShapeDtypeStruct((3 * B, ROWS), F32...]
    unnamed x7 -> x0, local copies, waits for them, and re-layouts: 5.33 us -> none
where the time goes in v2:
time: 131 us
  Pallas kernels  130 us (99%)
    pallas_call x1, Pallas kernels, local(): pl.pallas_call(kernel, out_shape=(jax.ShapeDtypeStruct((3 * B, ROWS), F32...  124 us
    pallas_call x1, Pallas kernels, local(): pl.pallas_call(finish, grid=(4,), out_shape=(jax.ShapeDtypeStruct((ROWS,...  5.53 us

profile of v2, /device:TPU:1, one launch (start us, length us, event | category | flops | bytes accessed | tf_op | source)
XLA Modules:
  0.0 130.6 jit_solution(15790419107621995153)
XLA Ops:
  0.6 124.5 %lanczos.1 = (f32[384,2048]{1,0:T(8,128)}, f32[128,384]{1,0:T(8,128)}, f32[384,256]{1,0:T(8,128)}, f32[384,256]{1,0:T(8,128)}) custom-call(s32[128]{0:T(128)} %seed.1, f32[2048,1024]{1,0:T(8,128)} %cov.1), custom_call_target="tpu_custom_call" | custom-call | tf_op jit(solution)/shard_map/lanczos/pallas_call | solution.py:534
  125.1 5.5 %finish.1 = (f32[2048,384]{1,0:T(8,128)}, f32[384,256]{1,0:T(8,128)}, f32[384,256]{1,0:T(8,128)}) custom-call(f32[384,2048]{1,0:T(8,128)} %get-tuple-element.7.p, f32[128,384]{1,0:T(8,128)} %get-tuple-element.8.l, f32[384,256]{1,0:T(8,128)} %get-tuple-element.9.h, f32[384,256]{1,0:T(8,128)} %get-tuple-element.10.f), custom_call_target="tpu_custom_call" | custom-call | tf_op jit(solution)/shard_map/finish/pallas_call | solution.py:549

commit v3 on v2

v3 whole, which is shorter than its diff:
```python
import jax
import jax.numpy as jnp
from jax import lax
from jax.experimental import pallas as pl
from jax.experimental.pallas import tpu as pltpu
from jax.sharding import PartitionSpec as P

N = 16384
B = 128
ITERS = 2
ROWS = 2048
COLS = 1024
NB = 16
MESH = pl.DeviceIdType.MESH
F32 = jnp.float32
BF16 = jnp.bfloat16
NN = (((1,), (0,)), ((), ()))
NT = (((1,), (1,)), ((), ()))
TN = (((0,), (0,)), ((), ()))


def exact(a, b, dims=NN):
    return lax.dot_general(a, b, dims, precision=lax.Precision.HIGHEST, preferred_element_type=F32)


def halves(a):
    high = a.astype(BF16)
    return high, (a - high.astype(F32)).astype(BF16)


def fine(a, b, dims=NN):
    ah, al = halves(a)
    bh, bl = halves(b)

    def dot(x, y):
        return lax.dot_general(x, y, dims, preferred_element_type=F32)

    both = dot(jnp.concatenate([ah, al], axis=0), bh)
    n = a.shape[0]
    return both[:n] + (both[n:] + dot(ah, bl))


def factor(gram, aug, low):
    rows = lax.broadcasted_iota(jnp.int32, (B, B), 0)
    lanes = lax.broadcasted_iota(jnp.int32, (B, B), 1)
    aug[:, :B] = gram
    aug[:, B:] = jnp.where(rows == lanes, 1.0, 0.0).astype(F32)
    lane = lax.broadcasted_iota(jnp.int32, (NB, B), 1)
    sub = lax.broadcasted_iota(jnp.int32, (NB, B), 0)

    def panel(p, carry):
        o = pl.multiple_of(p * NB, NB)
        left = aug[pl.ds(o, NB), :B]
        right = aug[pl.ds(o, NB), B:]
        cols = []
        for t in range(NB):
            one = jnp.sum(jnp.where(lane == o + t, left, 0.0), axis=1, keepdims=True)
            cols.append(jnp.broadcast_to(one, (NB, B)))
        for t in range(NB):
            inv = lax.rsqrt(cols[t][t : t + 1, :])
            scale = jnp.where(sub == t, inv, 1.0)
            ratio = jnp.where(sub > t, cols[t] * inv, 0.0)
            left = left * scale
            right = right * scale
            left = left - ratio * left[t : t + 1, :]
            right = right - ratio * right[t : t + 1, :]
            for u in range(t + 1, NB):
                cols[u] = cols[u] - ratio * (cols[u][t : t + 1, :] * inv)
        left = jnp.where(lane >= o, left, 0.0)
        low[pl.ds(o, NB), :B] = jnp.where(lane >= o + sub, left, 0.0)
        low[pl.ds(o, NB), B:] = right
        both = jnp.concatenate([left, right], axis=1)
        aug[...] = aug[...] - exact(left, both, TN)
        return carry

    lax.fori_loop(0, B // NB, panel, 0)


def kernel(
    seed, cov, p_out, l_out, h_out, f_out,
    cvm, chi, clo, stp, rs1, vcol, st, ypart, d2d, yown, rs2, yt, zt, pt, wt, y1p, rs3, tsh, last, projection, first_pass,
    scat, aug, low0, low1, low2, mix, ga, gb, ia, ib, ka, kb, xa1, xb1, xc1, xd1, xa3, xb3, xc3, xd3,
    csem, osem, rs1_s, rs1_r, ag1_s, ag1_r, t_s, t_r, d2d_s, d2d_r, rs2_s, rs2_r, ag_s, ag_r, fw_s, fw_r, rs3_s, rs3_r,
    sa_s, sa_r, sb_s, sb_r, sc_s, sc_r,
):
    r = lax.axis_index("row")
    c = lax.axis_index("col")
    core = lax.rem(c, 2)
    chip = lax.div(c, 2)
    partner = c + 1 - 2 * core
    there = (chip, core * 8 + r)
    origin = (lax.rem(c, 8), 2 * r + lax.div(c, 8))
    stays = jnp.logical_and(there[0] == r, there[1] == c)

    def loop(lo, hi, body):
        def run(i, carry):
            body(i)
            return carry

        lax.fori_loop(lo, hi, run, 0)

    def remote(src, dst, ssem, rsem, dev):
        return pltpu.make_async_remote_copy(src, dst, ssem, rsem, device_id=dev, device_id_type=MESH)

    def row_peer(k):
        return lax.rem(r + k, 8)

    def col_peer(k):
        return lax.rem(c + k, 16)

    def added(buf, n):
        total = buf[0]
        for i in range(1, n):
            total = total + buf[i]
        return total

    def block(i):
        return pl.ds(pl.multiple_of(i * B, B), B)

    def load(i):
        return pltpu.make_async_copy(cov.at[pl.ds(i * 256, 256)], cvm.at[pl.ds(i * 256, 256)], csem.at[0])

    loop(0, 8, lambda i: load(i).start())
    barrier = pltpu.get_barrier_semaphore()

    def greet(dev):
        pl.semaphore_signal(barrier, inc=1, device_id=dev, device_id_type=MESH)

    loop(1, 8, lambda k: greet((row_peer(k), c)))
    loop(1, 16, lambda k: greet((r, col_peer(k))))

    @pl.when(jnp.logical_not(stays))
    def _():
        greet(there)
        greet(origin)

    pltpu.make_async_copy(cov, cvm, csem.at[0]).wait()

    def gather(i):
        lines = []
        for t in range(8):
            at = seed[i * 8 + t] - r * ROWS
            inside = (at >= 0) & (at < ROWS)
            line = cvm[pl.ds(jnp.clip(at, 0, ROWS - 1), 1), :]
            lines.append(jnp.where(inside, line, 0.0))
        full = jnp.concatenate(lines, axis=0)
        for b in range(8):
            stp[b, pl.ds(pl.multiple_of(i * 8, 8), 8), :] = full[:, b * B : (b + 1) * B]

    loop(0, B // 8, gather)

    @pl.when(stays)
    def _():
        pl.semaphore_wait(barrier, 22)

    @pl.when(jnp.logical_not(stays))
    def _():
        pl.semaphore_wait(barrier, 24)

    def rs1_send(k):
        to = row_peer(k)
        remote(stp.at[to], rs1.at[r], rs1_s.at[0], rs1_r.at[0], (to, c)).start()

    loop(1, 8, rs1_send)

    def split(i):
        high, rest = halves(cvm[block(i), :])
        chi[lax.div(i, 2), lax.rem(i, 2)] = high
        clo[lax.div(i, 2), lax.rem(i, 2)] = rest

    loop(0, 16, split)

    def seven(src, dst, ssem, rsem):
        return remote(src.at[pl.ds(0, 7)], dst.at[pl.ds(0, 7)], ssem.at[0], rsem.at[0], (r, c))

    def row_sum(src, dst, ssem, rsem):
        seven(src, dst, ssem, rsem).wait_recv()
        dst[r] = src[r]
        return added(dst, 8)

    start = row_sum(stp, rs1, rs1_s, rs1_r)
    vcol[:, block(r)] = start
    tsh[0] = start

    def ag1(k):
        return remote(vcol.at[:, block(r)], vcol.at[:, block(r)], ag1_s.at[0], ag1_r.at[0], (row_peer(k), c))

    loop(1, 8, lambda k: ag1(k).start())

    def turn(tag, dst, at, dev):
        return remote(tsh.at[tag], dst.at[0:B, block(at)], t_s.at[tag], t_r.at[tag], dev)

    def turn_start(tag, dst):
        @pl.when(jnp.logical_not(stays))
        def _():
            turn(tag, dst, there[1], there).start()

    def turn_wait(tag, dst):
        @pl.when(jnp.logical_not(stays))
        def _():
            turn(tag, dst, c, there).wait_recv()

        @pl.when(stays)
        def _():
            dst[0:B, block(c)] = tsh[tag]

    turn_start(0, st)

    def ag1_all():
        return remote(vcol.at[:, pl.ds(0, 7 * B)], vcol.at[:, pl.ds(0, 7 * B)], ag1_s.at[0], ag1_r.at[0], (r, c))

    ag1_all().wait_recv()

    def gather_start(buf, tag):
        mine = buf.at[0:B, block(c)]

        def send(k):
            i = lax.rem(chip + k, 8)
            remote(mine, mine, ag_s.at[tag], ag_r.at[tag, chip], (r, 2 * i + core)).start()

        loop(1, 8, send)
        remote(mine, mine, fw_s.at[tag], fw_r.at[tag], (r, partner)).start()

    def gather_relay(buf, tag):
        def relay(k):
            i = lax.rem(chip + 8 - k, 8)
            got = buf.at[0:B, block(2 * i + core)]
            remote(got, got, ag_s.at[tag], ag_r.at[tag, i], (r, c)).wait_recv()
            remote(got, got, fw_s.at[tag], fw_r.at[tag], (r, partner)).start()

        loop(1, 8, relay)

    def gather_all(buf, n, ssem, rsem, tag):
        got = buf.at[0:B, pl.ds(0, n * B)]
        return remote(got, got, ssem.at[tag], rsem.at[tag], (r, c))

    def gather_wait(buf, tag):
        gather_all(buf, 8, fw_s, fw_r, tag).wait_recv()

    def gather_sent(buf, tag):
        gather_all(buf, 7, ag_s, fw_r, tag).wait_send()
        gather_all(buf, 8, fw_s, fw_r, tag).wait_send()

    def spread(out, at, n_peers, ssem, rsem, dev):
        loop(1, n_peers, lambda k: remote(out.at[at], out.at[at], ssem, rsem, dev(k)).start())

    def rest(out, n_peers, ssem, rsem):
        got = out.at[pl.ds(0, n_peers - 1)]
        return remote(got, got, ssem, rsem, (r, c))

    def collect(out, n_peers, ssem, rsem):
        rest(out, n_peers, ssem, rsem).wait_recv()

    def over_row(k):
        return (row_peer(k), c)

    def over_col(k):
        return (r, col_peer(k))

    wides = {1: (xa1, xb1, xc1, xd1), 3: (xa3, xb3, xc3, xd3)}

    def wide_start(value, tag):
        a, b = wides[tag][:2]
        a[...] = value.reshape(8, 16, B)

        def send(k):
            to = row_peer(k)
            remote(a.at[to], b.at[r], sa_s.at[tag], sa_r.at[tag], (to, c)).start()

        loop(1, 8, send)

    def wide_second(tag):
        a, b, d = wides[tag][:3]
        collect(b, 8, sa_s.at[tag], sa_r.at[tag])
        b[r] = a[r]
        d[c] = added(b, 8)
        spread(d, c, 16, sb_s.at[tag], sb_r.at[tag], over_col)

    def wide_third(tag):
        d, e = wides[tag][2:]
        collect(d, 16, sb_s.at[tag], sb_r.at[tag])
        e[r] = added(d, 16)
        spread(e, r, 8, sc_s.at[tag], sc_r.at[tag], over_row)

    def wide_end(tag):
        e = wides[tag][3]
        collect(e, 8, sc_s.at[tag], sc_r.at[tag])
        return e[...].reshape(B, B)

    ga[c] = fine(vcol[pl.ds(pl.multiple_of(r * 16, 16), 16), :], vcol[...], NT)
    spread(ga, c, 16, sb_s.at[0], sb_r.at[0], over_col)

    def cat(i):
        high, rest = halves(vcol[:, block(i)].T)
        scat[block(i), :B] = high
        scat[block(i), B:] = rest

    loop(0, 8, cat)

    def times(first, parity):
        a = chi[pl.ds(first, 4), parity].reshape(512, COLS)
        b = clo[pl.ds(first, 4), parity].reshape(512, COLS)
        full = jnp.dot(a, scat[...], preferred_element_type=F32) + jnp.dot(b, scat[...], preferred_element_type=F32)
        return (full[:, :B] + full[:, B:]).reshape(4, B, B)

    def across(h):
        return remote(ypart.at[pl.ds(h * 4, 4)], d2d.at[pl.ds(h * 4, 4)], d2d_s.at[h], d2d_r.at[h], (r, partner))

    def theirs(h):
        ypart[pl.ds(h * 4, 4)] = times(h * 4, 1 - core)
        across(h).start()

    loop(0, 2, theirs)
    turn_wait(0, st)
    gather_start(st, 0)

    def ours(h):
        yown[pl.ds(h * 4, 4)] = times(h * 4, core)

    loop(0, 2, ours)

    def rs2_copy(i):
        return remote(yown.at[i], rs2.at[chip], rs2_s.at[0], rs2_r.at[0], (r, 2 * i + core))

    def combine(h):
        across(h).wait_recv()
        for t in range(4):
            i = h * 4 + t
            yown[i] = yown[i] + d2d[i]

            @pl.when(i != chip)
            def _():
                rs2_copy(i).start()

    loop(0, 2, combine)

    collect(ga, 16, sb_s.at[0], sb_r.at[0])
    gb[r] = added(ga, 16)
    spread(gb, r, 8, sc_s.at[0], sc_r.at[0], over_row)
    gather_relay(st, 0)

    seven(yown, rs2, rs2_s, rs2_r).wait_recv()
    rs2[chip] = yown[chip]
    fresh = added(rs2, 8).T
    yt[:, block(c)] = fresh
    wide_start(exact(st[:, block(c)], fresh, NT), 1)
    gather_start(yt, 1)

    collect(gb, 8, sc_s.at[0], sc_r.at[0])
    factor(gb[...].reshape(B, B), aug, low0)
    inv0 = low0[:, B:]
    wide_second(1)
    gather_wait(st, 0)

    def put(i):
        return pltpu.make_async_copy(pt.at[pl.ds(i * B, B)], p_out.at[pl.ds(i * B, B)], osem.at[0])

    def first_q(i):
        o = pl.ds(pl.multiple_of(i * 512, 512), 512)
        pt[0:B, o] = fine(inv0, st[:, o])

    loop(0, 4, first_q)
    put(0).start()
    gather_relay(yt, 1)
    wide_third(1)
    gather_wait(yt, 1)

    def small_start(value, buf, tag):
        buf[r] = value
        spread(buf, r, 8, sa_s.at[tag], sa_r.at[tag], over_row)

    def small_middle(buf, out, tag):
        collect(buf, 8, sa_s.at[tag], sa_r.at[tag])
        out[c] = added(buf, 8)
        spread(out, c, 16, sb_s.at[tag], sb_r.at[tag], over_col)

    def small_end(out, n, tag):
        collect(out, 16, sb_s.at[tag], sb_r.at[tag])
        return out[...].reshape(16 * n, B)

    def share(n):
        return pl.ds(pl.multiple_of(c * n, 8), n)

    def first_image(i):
        o = pl.ds(pl.multiple_of(i * 512, 512), 512)
        pt[2 * B : 3 * B, o] = fine(inv0, yt[:, o])

    loop(0, 4, first_image)
    first_pass[...] = jnp.zeros((3 * B, 2 * B), F32)
    projection[...] = jnp.zeros((3 * B, 2 * B), F32)
    h1 = exact(exact(inv0, wide_end(1)), inv0, NT)
    first_pass[0:B, 0:B] = h1
    h1t = h1.T

    def once(i):
        o = pl.ds(pl.multiple_of(i * 512, 512), 512)
        w = pt[2 * B : 3 * B, o] - fine(h1t, pt[0:B, o])
        pt[B : 2 * B, o] = w
        high, rest = halves(w)
        wt[0:B, o] = high
        wt[B : 2 * B, o] = rest

    loop(0, 4, once)

    tsh[2] = pt[B : 2 * B, block(c)]

    @pl.when(jnp.logical_not(stays))
    def _():
        remote(tsh.at[2], tsh.at[3], t_s.at[2], t_r.at[2], origin).start()

    def times_t(k):
        q = lax.rem(lax.div(r, 2) + 1 + k, 4)
        o = pl.ds(pl.multiple_of(q * 256, 256), 256)
        a = chi[:, :, :, o].reshape(ROWS, 256)
        b = clo[:, :, :, o].reshape(ROWS, 256)
        full = jnp.dot(wt[...], a, preferred_element_type=F32) + jnp.dot(wt[...], b, preferred_element_type=F32)
        half = full[:B, :] + full[B:, :]
        y1p[2 * q] = half[:, :B]
        y1p[2 * q + 1] = half[:, B:]
        for t in range(2):
            to = 2 * q + t

            @pl.when(to != r)
            def _():
                remote(y1p.at[to], rs3.at[r], rs3_s.at[0], rs3_r.at[0], (to, c)).start()

    loop(0, 4, times_t)

    small_start(fine(pt[share(24), :], pt[B : 2 * B, :], NT), ia, 2)
    fresh1 = row_sum(y1p, rs3, rs3_s, rs3_r)
    tsh[1] = fresh1
    turn_start(1, zt)

    @pl.when(jnp.logical_not(stays))
    def _():
        remote(tsh.at[2], tsh.at[3], t_s.at[2], t_r.at[2], origin).wait_recv()

    @pl.when(stays)
    def _():
        tsh[3] = tsh[2]

    wide_start(exact(tsh[3], tsh[1], NT), 3)
    small_middle(ia, ib, 2)
    wide_second(3)
    turn_wait(1, zt)
    gather_start(zt, 2)
    sums = small_end(ib, 24, 2)
    h2 = sums[0:B, :]
    h2t = h2.T
    crossed = sums[2 * B : 3 * B, :]
    projection[0:B, 0:B] = h1 + h2
    factor(sums[B : 2 * B, :] - exact(h2t, h2), aug, low1)
    projection[B : 2 * B, 0:B] = low1[:, :B]
    inv1 = low1[:, B:]
    wide_third(3)
    tail = exact(inv1, h2t)
    mix1 = jnp.concatenate([-tail, inv1], axis=1)
    gather_relay(zt, 2)

    def second_q(i):
        o = pl.ds(pl.multiple_of(i * 512, 512), 512)
        pt[B : 2 * B, o] = fine(mix1, pt[0 : 2 * B, o])

    loop(0, 4, second_q)
    put(1).start()

    top = exact(crossed - exact(h1t, h2), inv1, NT)
    bent = exact(h2t, crossed - exact(h1, h2) * 0.5)
    below = exact(exact(inv1, wide_end(3) - bent - bent.T), inv1, NT)
    first_pass[0:B, B : 2 * B] = top
    first_pass[B : 2 * B, B : 2 * B] = below
    passed = pltpu.make_async_copy(first_pass, f_out, osem.at[1])
    passed.start()
    mix[...] = jnp.concatenate([inv1, -top.T, -below.T, -tail], axis=1)
    gather_wait(zt, 2)

    def once1(i):
        o = pl.ds(pl.multiple_of(i * 512, 512), 512)
        pt[2 * B : 3 * B, o] = fine(mix[...], jnp.concatenate([zt[:, o], pt[:, o]], axis=0))

    loop(0, 4, once1)
    put(2).start()
    small_start(fine(pt[share(24), :], pt[2 * B : 3 * B, :], NT), ka, 4)
    small_middle(ka, kb, 4)
    sums1 = small_end(kb, 24, 4)
    h2b = sums1[0 : 2 * B, :]
    projection[0:B, B : 2 * B] = top + h2b[0:B]
    projection[B : 2 * B, B : 2 * B] = below + h2b[B:]
    factor(sums1[2 * B : 3 * B, :] - exact(h2b, h2b, TN), aug, low2)
    projection[2 * B : 3 * B, B : 2 * B] = low2[:, :B]
    inv2 = low2[:, B:]
    projected = pltpu.make_async_copy(projection, h_out, osem.at[2])
    projected.start()
    last[...] = jnp.concatenate([-exact(inv2, h2b, NT), inv2], axis=1)
    mixed = pltpu.make_async_copy(last, l_out, osem.at[3])
    mixed.start()

    seven(stp, rs1, rs1_s, rs1_r).wait_send()
    seven(yown, rs2, rs2_s, rs2_r).wait_send()
    seven(y1p, rs3, rs3_s, rs3_r).wait_send()
    ag1_all().wait_send()

    @pl.when(jnp.logical_not(stays))
    def _():
        for tag in range(3):
            turn(tag, zt, c, there).wait_send()

    loop(0, 2, lambda h: across(h).wait_send())
    for tag, buf in enumerate((st, yt, zt)):
        gather_sent(buf, tag)
    rest(ga, 16, sb_s.at[0], sb_r.at[0]).wait_send()
    rest(gb, 8, sc_s.at[0], sc_r.at[0]).wait_send()
    for tag, (a, b) in ((2, (ia, ib)), (4, (ka, kb))):
        rest(a, 8, sa_s.at[tag], sa_r.at[tag]).wait_send()
        rest(b, 16, sb_s.at[tag], sb_r.at[tag]).wait_send()
    for tag in (1, 3):
        rest(wides[tag][0], 8, sa_s.at[tag], sa_r.at[tag]).wait_send()
        rest(wides[tag][2], 16, sb_s.at[tag], sb_r.at[tag]).wait_send()
        rest(wides[tag][3], 8, sc_s.at[tag], sc_r.at[tag]).wait_send()
    pltpu.make_async_copy(pt, p_out, osem.at[0]).wait()
    passed.wait()
    projected.wait()
    mixed.wait()


def finish(p, l, h, f, basis, projection, first_pass):
    basis[:, : 2 * B] = p[: 2 * B, :].T * F32(N**0.5)
    basis[:, 2 * B :] = fine(l[...], p[...]).T * F32(N**0.5)
    projection[...] = h[...]
    first_pass[...] = f[...]


def local(covariance, seed_index):
    v = pltpu.VMEM
    dma = pltpu.SemaphoreType.DMA
    blocks8 = v((8, B, B), F32)
    wide = v((B, ROWS), F32)
    square = v((B, 2 * B), F32)
    small = [v((16, 16, B), F32), v((8, 16, B), F32)]
    for n in (24, 24):
        small += [v((8, n, B), F32), v((16, n, B), F32)]
    thin8, thin16 = v((8, 16, B), F32), v((16, 16, B), F32)
    scratch = [
        v((ROWS, COLS), F32), v((8, 2, B, COLS), BF16), v((8, 2, B, COLS), BF16),
        blocks8, blocks8, v((B, COLS), F32), wide,
        blocks8, blocks8, blocks8, blocks8, wide,
        wide, v((3 * B, ROWS), F32), v((2 * B, ROWS), BF16), blocks8, blocks8, v((4, B, B), F32),
        v((B, 3 * B), F32), v((3 * B, 2 * B), F32), v((3 * B, 2 * B), F32),
        v((COLS, 2 * B), BF16), square, square, square, square, v((B, 4 * B), F32), *small,
        *(thin8, thin8, thin16, thin8) * 2,
        dma((1,)), dma((4,)), dma((1,)), dma((1,)), dma((1,)), dma((1,)), dma((3,)), dma((3,)),
        dma((2,)), dma((2,)), dma((1,)), dma((1,)), dma((3,)), dma((3, 8)), dma((3,)), dma((3,)), dma((1,)), dma((1,)),
        dma((5,)), dma((5,)), dma((5,)), dma((5,)), dma((5,)), dma((5,)),
    ]
    any_space = pl.BlockSpec(memory_space=pl.ANY)
    wide_p, mixed, square_h, square_f = pl.pallas_call(
        kernel,
        out_shape=(
            jax.ShapeDtypeStruct((3 * B, ROWS), F32),
            jax.ShapeDtypeStruct((B, 3 * B), F32),
            jax.ShapeDtypeStruct((3 * B, 2 * B), F32),
            jax.ShapeDtypeStruct((3 * B, 2 * B), F32),
        ),
        in_specs=[pl.BlockSpec(memory_space=pltpu.SMEM), any_space],
        out_specs=[any_space] * 4,
        scratch_shapes=scratch,
        compiler_params=pltpu.CompilerParams(collective_id=0, has_side_effects=True, vmem_limit_bytes=60 * 2**20),
        name="lanczos",
    )(seed_index, covariance)
    whole = pl.BlockSpec((3 * B, 2 * B), lambda i: (0, 0))
    return pl.pallas_call(
        finish,
        grid=(4,),
        out_shape=(
            jax.ShapeDtypeStruct((ROWS, 3 * B), F32),
            jax.ShapeDtypeStruct((3 * B, 2 * B), F32),
            jax.ShapeDtypeStruct((3 * B, 2 * B), F32),
        ),
        in_specs=[pl.BlockSpec((3 * B, 512), lambda i: (0, i)), pl.BlockSpec((B, 3 * B), lambda i: (0, 0)), whole, whole],
        out_specs=(pl.BlockSpec((512, 3 * B), lambda i: (i, 0)), whole, whole),
        name="finish",
    )(wide_p, mixed, square_h, square_f)


def solution(mesh):
    return jax.shard_map(
        local,
        mesh=mesh,
        in_specs=(P("row", "col"), P()),
        out_specs=(P("row", None), P(), P()),
        check_vma=False,
    )
```

time: 131 us -> 116 us (0.89)
  Pallas kernels: 130 us -> 116 us
    pallas_call x1, Pallas kernels: 124 us -> 110 us  [local(): pl.pallas_call(kernel, out_shape=(jax.ShapeDtypeStruct((3 * B, ROWS), F32...]
where the time goes in v3:
time: 116 us
  Pallas kernels  116 us (100%)
    pallas_call x1, Pallas kernels, local(): pl.pallas_call(kernel, out_shape=(jax.ShapeDtypeStruct((3 * B, ROWS), F32...  110 us
    pallas_call x1, Pallas kernels, local(): pl.pallas_call(finish, grid=(4,), out_shape=(jax.ShapeDtypeStruct((ROWS,...  5.53 us

profile of v3, /device:TPU:1, one launch (start us, length us, event | category | flops | bytes accessed | tf_op | source)
XLA Modules:
  0.0 116.3 jit_solution(14122966793280285674)
XLA Ops:
  0.6 110.1 %lanczos.1 = (f32[384,2048]{1,0:T(8,128)}, f32[128,384]{1,0:T(8,128)}, f32[384,256]{1,0:T(8,128)}, f32[384,256]{1,0:T(8,128)}) custom-call(s32[128]{0:T(128)} %seed.1, f32[2048,1024]{1,0:T(8,128)} %cov.1), custom_call_target="tpu_custom_call" | custom-call | tf_op jit(solution)/shard_map/lanczos/pallas_call | solution.py:556
  110.8 5.5 %finish.1 = (f32[2048,384]{1,0:T(8,128)}, f32[384,256]{1,0:T(8,128)}, f32[384,256]{1,0:T(8,128)}) custom-call(f32[384,2048]{1,0:T(8,128)} %get-tuple-element.7.p, f32[128,384]{1,0:T(8,128)} %get-tuple-element.8.l, f32[384,256]{1,0:T(8,128)} %get-tuple-element.9.h, f32[384,256]{1,0:T(8,128)} %get-tuple-element.10.f), custom_call_target="tpu_custom_call" | custom-call | tf_op jit(solution)/shard_map/finish/pallas_call | solution.py:571

commit v4 on v3

--- a/solution.py
+++ b/solution.py
@@ -40,11 +40,14 @@
     return both[:n] + (both[n:] + dot(ah, bl))
 
 
-def factor(gram, aug, low):
+def factor_start(gram, aug):
     rows = lax.broadcasted_iota(jnp.int32, (B, B), 0)
     lanes = lax.broadcasted_iota(jnp.int32, (B, B), 1)
     aug[:, :B] = gram
     aug[:, B:] = jnp.where(rows == lanes, 1.0, 0.0).astype(F32)
+
+
+def factor_half(aug, low, half):
     lane = lax.broadcasted_iota(jnp.int32, (NB, B), 1)
     sub = lax.broadcasted_iota(jnp.int32, (NB, B), 0)
 
@@ -73,7 +76,7 @@
         aug[...] = aug[...] - exact(left, both, TN)
         return carry
 
-    lax.fori_loop(0, B // NB, panel, 0)
+    lax.fori_loop(half * (B // NB // 2), (half + 1) * (B // NB // 2), panel, 0)
 
 
 def kernel(
@@ -185,7 +188,6 @@
     def ag1(k):
         return remote(vcol.at[:, block(r)], vcol.at[:, block(r)], ag1_s.at[0], ag1_r.at[0], (row_peer(k), c))
 
-    loop(1, 8, lambda k: ag1(k).start())
 
     def turn(tag, dst, at, dev):
         return remote(tsh.at[tag], dst.at[0:B, block(at)], t_s.at[tag], t_r.at[tag], dev)
@@ -204,12 +206,10 @@
         def _():
             dst[0:B, block(c)] = tsh[tag]
 
-    turn_start(0, st)
 
     def ag1_all():
         return remote(vcol.at[:, pl.ds(0, 7 * B)], vcol.at[:, pl.ds(0, 7 * B)], ag1_s.at[0], ag1_r.at[0], (r, c))
 
-    ag1_all().wait_recv()
 
     def gather_start(buf, tag):
         mine = buf.at[0:B, block(c)]
@@ -287,6 +287,12 @@
         collect(e, 8, sc_s.at[tag], sc_r.at[tag])
         return e[...].reshape(B, B)
 
+    turn_start(0, st)
+    loop(1, 8, lambda k: ag1(k).start())
+    turn_wait(0, st)
+    gather_start(st, 0)
+    ag1_all().wait_recv()
+
     ga[c] = fine(vcol[pl.ds(pl.multiple_of(r * 16, 16), 16), :], vcol[...], NT)
     spread(ga, c, 16, sb_s.at[0], sb_r.at[0], over_col)
 
@@ -311,8 +317,6 @@
         across(h).start()
 
     loop(0, 2, theirs)
-    turn_wait(0, st)
-    gather_start(st, 0)
 
     def ours(h):
         yown[pl.ds(h * 4, 4)] = times(h * 4, core)
@@ -334,35 +338,43 @@
 
     loop(0, 2, combine)
 
+    gather_relay(st, 0)
+    gather_wait(st, 0)
+
+    bent0 = fine(st[:, block(core)], yown[0])
+    for i in range(1, 8):
+        bent0 = bent0 + fine(st[:, block(2 * i + core)], yown[i])
+    wide_start(bent0, 1)
+
     collect(ga, 16, sb_s.at[0], sb_r.at[0])
     gb[r] = added(ga, 16)
     spread(gb, r, 8, sc_s.at[0], sc_r.at[0], over_row)
-    gather_relay(st, 0)
 
     seven(yown, rs2, rs2_s, rs2_r).wait_recv()
     rs2[chip] = yown[chip]
-    fresh = added(rs2, 8).T
-    yt[:, block(c)] = fresh
-    wide_start(exact(st[:, block(c)], fresh, NT), 1)
+    yt[:, block(c)] = added(rs2, 8).T
+    wide_second(1)
     gather_start(yt, 1)
 
     collect(gb, 8, sc_s.at[0], sc_r.at[0])
-    factor(gb[...].reshape(B, B), aug, low0)
+    factor_start(gb[...].reshape(B, B), aug)
+    factor_half(aug, low0, 0)
+    factor_half(aug, low0, 1)
+    wide_third(1)
     inv0 = low0[:, B:]
-    wide_second(1)
-    gather_wait(st, 0)
 
     def put(i):
         return pltpu.make_async_copy(pt.at[pl.ds(i * B, B)], p_out.at[pl.ds(i * B, B)], osem.at[0])
 
     def first_q(i):
-        o = pl.ds(pl.multiple_of(i * 512, 512), 512)
+        o = pl.ds(i * 512, 512)
         pt[0:B, o] = fine(inv0, st[:, o])
 
-    loop(0, 4, first_q)
+    for i in range(4):
+        first_q(i)
+
     put(0).start()
     gather_relay(yt, 1)
-    wide_third(1)
     gather_wait(yt, 1)
 
     def small_start(value, buf, tag):
@@ -382,10 +394,12 @@
         return pl.ds(pl.multiple_of(c * n, 8), n)
 
     def first_image(i):
-        o = pl.ds(pl.multiple_of(i * 512, 512), 512)
+        o = pl.ds(i * 512, 512)
         pt[2 * B : 3 * B, o] = fine(inv0, yt[:, o])
 
-    loop(0, 4, first_image)
+    for i in range(4):
+        first_image(i)
+
     first_pass[...] = jnp.zeros((3 * B, 2 * B), F32)
     projection[...] = jnp.zeros((3 * B, 2 * B), F32)
     h1 = exact(exact(inv0, wide_end(1)), inv0, NT)
@@ -393,14 +407,16 @@
     h1t = h1.T
 
     def once(i):
-        o = pl.ds(pl.multiple_of(i * 512, 512), 512)
+        o = pl.ds(i * 512, 512)
         w = pt[2 * B : 3 * B, o] - fine(h1t, pt[0:B, o])
         pt[B : 2 * B, o] = w
         high, rest = halves(w)
         wt[0:B, o] = high
         wt[B : 2 * B, o] = rest
 
-    loop(0, 4, once)
+    for i in range(4):
+        once(i)
+
 
     tsh[2] = pt[B : 2 * B, block(c)]
 
@@ -449,25 +465,29 @@
     h2t = h2.T
     crossed = sums[2 * B : 3 * B, :]
     projection[0:B, 0:B] = h1 + h2
-    factor(sums[B : 2 * B, :] - exact(h2t, h2), aug, low1)
+    factor_start(sums[B : 2 * B, :] - exact(h2t, h2), aug)
+    factor_half(aug, low1, 0)
+    wide_third(3)
+    factor_half(aug, low1, 1)
     projection[B : 2 * B, 0:B] = low1[:, :B]
     inv1 = low1[:, B:]
-    wide_third(3)
     tail = exact(inv1, h2t)
     mix1 = jnp.concatenate([-tail, inv1], axis=1)
-    gather_relay(zt, 2)
 
     def second_q(i):
-        o = pl.ds(pl.multiple_of(i * 512, 512), 512)
+        o = pl.ds(i * 512, 512)
         pt[B : 2 * B, o] = fine(mix1, pt[0 : 2 * B, o])
 
-    loop(0, 4, second_q)
+    for i in range(4):
+        second_q(i)
+
     put(1).start()
 
     top = exact(crossed - exact(h1t, h2), inv1, NT)
     bent = exact(h2t, crossed - exact(h1, h2) * 0.5)
+    first_pass[0:B, B : 2 * B] = top
+    gather_relay(zt, 2)
     below = exact(exact(inv1, wide_end(3) - bent - bent.T), inv1, NT)
-    first_pass[0:B, B : 2 * B] = top
     first_pass[B : 2 * B, B : 2 * B] = below
     passed = pltpu.make_async_copy(first_pass, f_out, osem.at[1])
     passed.start()
@@ -475,10 +495,12 @@
     gather_wait(zt, 2)
 
     def once1(i):
-        o = pl.ds(pl.multiple_of(i * 512, 512), 512)
+        o = pl.ds(i * 512, 512)
         pt[2 * B : 3 * B, o] = fine(mix[...], jnp.concatenate([zt[:, o], pt[:, o]], axis=0))
 
-    loop(0, 4, once1)
+    for i in range(4):
+        once1(i)
+
     put(2).start()
     small_start(fine(pt[share(24), :], pt[2 * B : 3 * B, :], NT), ka, 4)
     small_middle(ka, kb, 4)
@@ -486,7 +508,9 @@
     h2b = sums1[0 : 2 * B, :]
     projection[0:B, B : 2 * B] = top + h2b[0:B]
     projection[B : 2 * B, B : 2 * B] = below + h2b[B:]
-    factor(sums1[2 * B : 3 * B, :] - exact(h2b, h2b, TN), aug, low2)
+    factor_start(sums1[2 * B : 3 * B, :] - exact(h2b, h2b, TN), aug)
+    factor_half(aug, low2, 0)
+    factor_half(aug, low2, 1)
     projection[2 * B : 3 * B, B : 2 * B] = low2[:, :B]
     inv2 = low2[:, B:]
     projected = pltpu.make_async_copy(projection, h_out, osem.at[2])
@@ -570,14 +594,14 @@
     whole = pl.BlockSpec((3 * B, 2 * B), lambda i: (0, 0))
     return pl.pallas_call(
         finish,
-        grid=(4,),
+        grid=(2,),
         out_shape=(
             jax.ShapeDtypeStruct((ROWS, 3 * B), F32),
             jax.ShapeDtypeStruct((3 * B, 2 * B), F32),
             jax.ShapeDtypeStruct((3 * B, 2 * B), F32),
         ),
-        in_specs=[pl.BlockSpec((3 * B, 512), lambda i: (0, i)), pl.BlockSpec((B, 3 * B), lambda i: (0, 0)), whole, whole],
-        out_specs=(pl.BlockSpec((512, 3 * B), lambda i: (i, 0)), whole, whole),
+        in_specs=[pl.BlockSpec((3 * B, ROWS // 2), lambda i: (0, i)), pl.BlockSpec((B, 3 * B), lambda i: (0, 0)), whole, whole],
+        out_specs=(pl.BlockSpec((ROWS // 2, 3 * B), lambda i: (i, 0)), whole, whole),
         name="finish",
     )(wide_p, mixed, square_h, square_f)
 

time: 116 us -> 110 us (0.948)
  Pallas kernels: 116 us -> 110 us
    pallas_call x1, Pallas kernels: 110 us -> 105 us  [local(): pl.pallas_call(kernel, out_shape=(jax.ShapeDtypeStruct((3 * B, ROWS), F32...]
where the time goes in v4:
time: 110 us
  Pallas kernels  110 us (100%)
    pallas_call x1, Pallas kernels, local(): pl.pallas_call(kernel, out_shape=(jax.ShapeDtypeStruct((3 * B, ROWS), F32...  105 us
    pallas_call x1, Pallas kernels, local(): pl.pallas_call(finish, grid=(2,), out_shape=(jax.ShapeDtypeStruct((ROWS,...  4.41 us

profile of v4, /device:TPU:1, one launch (start us, length us, event | category | flops | bytes accessed | tf_op | source)
XLA Modules:
  0.0 110.1 jit_solution(5057094904812688029)
XLA Ops:
  0.6 105.1 %lanczos.1 = (f32[384,2048]{1,0:T(8,128)}, f32[128,384]{1,0:T(8,128)}, f32[384,256]{1,0:T(8,128)}, f32[384,256]{1,0:T(8,128)}) custom-call(s32[128]{0:T(128)} %seed.1, f32[2048,1024]{1,0:T(8,128)} %cov.1), custom_call_target="tpu_custom_call" | custom-call | tf_op jit(solution)/shard_map/lanczos/pallas_call | solution.py:580
  105.7 4.4 %finish.1 = (f32[2048,384]{1,0:T(8,128)}, f32[384,256]{1,0:T(8,128)}, f32[384,256]{1,0:T(8,128)}) custom-call(f32[384,2048]{1,0:T(8,128)} %get-tuple-element.7.p, f32[128,384]{1,0:T(8,128)} %get-tuple-element.8.l, f32[384,256]{1,0:T(8,128)} %get-tuple-element.9.h, f32[384,256]{1,0:T(8,128)} %get-tuple-element.10.f), custom_call_target="tpu_custom_call" | custom-call | tf_op jit(solution)/shard_map/finish/pallas_call | solution.py:595

commit v5 on v4

--- a/solution.py
+++ b/solution.py
@@ -19,13 +19,24 @@
 TN = (((0,), (0,)), ((), ()))
 
 
-def exact(a, b, dims=NN):
-    return lax.dot_general(a, b, dims, precision=lax.Precision.HIGHEST, preferred_element_type=F32)
-
-
 def halves(a):
     high = a.astype(BF16)
     return high, (a - high.astype(F32)).astype(BF16)
+
+
+def exact(a, b, dims=NN):
+    def thirds(x):
+        high = x.astype(BF16)
+        rest = x - high.astype(F32)
+        middle = rest.astype(BF16)
+        return high, middle, (rest - middle.astype(F32)).astype(BF16)
+
+    (over_a,), (over_b,) = dims[0]
+    ah, am, al = thirds(a)
+    bh, bm, bl = thirds(b)
+    left = jnp.concatenate([al, am, ah, am, ah, ah], axis=over_a)
+    right = jnp.concatenate([bh, bm, bl, bh, bm, bh], axis=over_b)
+    return lax.dot_general(left, right, dims, preferred_element_type=F32)
 
 
 def fine(a, b, dims=NN):
@@ -186,7 +197,7 @@
     tsh[0] = start
 
     def ag1(k):
-        return remote(vcol.at[:, block(r)], vcol.at[:, block(r)], ag1_s.at[0], ag1_r.at[0], (row_peer(k), c))
+        return remote(vcol.at[:, block(r)], vcol.at[:, block(r)], ag1_s.at[0], ag1_r.at[r], (row_peer(k), c))
 
 
     def turn(tag, dst, at, dev):
@@ -207,9 +218,8 @@
             dst[0:B, block(c)] = tsh[tag]
 
 
-    def ag1_all():
+    def ag1_sent():
         return remote(vcol.at[:, pl.ds(0, 7 * B)], vcol.at[:, pl.ds(0, 7 * B)], ag1_s.at[0], ag1_r.at[0], (r, c))
-
 
     def gather_start(buf, tag):
         mine = buf.at[0:B, block(c)]
@@ -291,17 +301,22 @@
     loop(1, 8, lambda k: ag1(k).start())
     turn_wait(0, st)
     gather_start(st, 0)
-    ag1_all().wait_recv()
-
-    ga[c] = fine(vcol[pl.ds(pl.multiple_of(r * 16, 16), 16), :], vcol[...], NT)
-    spread(ga, c, 16, sb_s.at[0], sb_r.at[0], over_col)
-
     def cat(i):
         high, rest = halves(vcol[:, block(i)].T)
         scat[block(i), :B] = high
         scat[block(i), B:] = rest
 
-    loop(0, 8, cat)
+    cat(r)
+
+    def ag1_wait(k):
+        i = lax.rem(r + 8 - k, 8)
+        remote(vcol.at[:, block(i)], vcol.at[:, block(i)], ag1_s.at[0], ag1_r.at[i], (r, c)).wait_recv()
+        cat(i)
+
+    loop(1, 8, ag1_wait)
+
+    ga[c] = fine(vcol[pl.ds(pl.multiple_of(r * 16, 16), 16), :], vcol[...], NT)
+    spread(ga, c, 16, sb_s.at[0], sb_r.at[0], over_col)
 
     def times(first, parity):
         a = chi[pl.ds(first, 4), parity].reshape(512, COLS)
@@ -339,7 +354,6 @@
     loop(0, 2, combine)
 
     gather_relay(st, 0)
-    gather_wait(st, 0)
 
     bent0 = fine(st[:, block(core)], yown[0])
     for i in range(1, 8):
@@ -362,6 +376,8 @@
     factor_half(aug, low0, 1)
     wide_third(1)
     inv0 = low0[:, B:]
+
+    gather_wait(st, 0)
 
     def put(i):
         return pltpu.make_async_copy(pt.at[pl.ds(i * B, B)], p_out.at[pl.ds(i * B, B)], osem.at[0])
@@ -429,8 +445,8 @@
         o = pl.ds(pl.multiple_of(q * 256, 256), 256)
         a = chi[:, :, :, o].reshape(ROWS, 256)
         b = clo[:, :, :, o].reshape(ROWS, 256)
-        full = jnp.dot(wt[...], a, preferred_element_type=F32) + jnp.dot(wt[...], b, preferred_element_type=F32)
-        half = full[:B, :] + full[B:, :]
+        full = jnp.dot(wt[...], a, preferred_element_type=F32)
+        half = full[:B, :] + (full[B:, :] + jnp.dot(wt[0:B, :], b, preferred_element_type=F32))
         y1p[2 * q] = half[:, :B]
         y1p[2 * q + 1] = half[:, B:]
         for t in range(2):
@@ -522,7 +538,7 @@
     seven(stp, rs1, rs1_s, rs1_r).wait_send()
     seven(yown, rs2, rs2_s, rs2_r).wait_send()
     seven(y1p, rs3, rs3_s, rs3_r).wait_send()
-    ag1_all().wait_send()
+    ag1_sent().wait_send()
 
     @pl.when(jnp.logical_not(stays))
     def _():
@@ -572,7 +588,7 @@
         v((B, 3 * B), F32), v((3 * B, 2 * B), F32), v((3 * B, 2 * B), F32),
         v((COLS, 2 * B), BF16), square, square, square, square, v((B, 4 * B), F32), *small,
         *(thin8, thin8, thin16, thin8) * 2,
-        dma((1,)), dma((4,)), dma((1,)), dma((1,)), dma((1,)), dma((1,)), dma((3,)), dma((3,)),
+        dma((1,)), dma((4,)), dma((1,)), dma((1,)), dma((1,)), dma((8,)), dma((3,)), dma((3,)),
         dma((2,)), dma((2,)), dma((1,)), dma((1,)), dma((3,)), dma((3, 8)), dma((3,)), dma((3,)), dma((1,)), dma((1,)),
         dma((5,)), dma((5,)), dma((5,)), dma((5,)), dma((5,)), dma((5,)),
     ]

time: 110 us -> 109 us (level)
  Pallas kernels: 110 us -> 108 us
    pallas_call x1, Pallas kernels: 105 us -> 103 us  [local(): pl.pallas_call(kernel, out_shape=(jax.ShapeDtypeStruct((3 * B, ROWS), F32...]
where the time goes in v5:
time: 109 us; the launch traced here: 108 us
  Pallas kernels  108 us (99%)
    pallas_call x1, Pallas kernels, local(): pl.pallas_call(kernel, out_shape=(jax.ShapeDtypeStruct((3 * B, ROWS), F32...  103 us
    pallas_call x1, Pallas kernels, local(): pl.pallas_call(finish, grid=(2,), out_shape=(jax.ShapeDtypeStruct((ROWS,...  4.41 us

profile of v5, /device:TPU:1, one launch (start us, length us, event | category | flops | bytes accessed | tf_op | source)
XLA Modules:
  0.0 108.5 jit_solution(17262677945374768437)
XLA Ops:
  0.6 103.4 %lanczos.1 = (f32[384,2048]{1,0:T(8,128)}, f32[128,384]{1,0:T(8,128)}, f32[384,256]{1,0:T(8,128)}, f32[384,256]{1,0:T(8,128)}) custom-call(s32[128]{0:T(128)} %seed.1, f32[2048,1024]{1,0:T(8,128)} %cov.1), custom_call_target="tpu_custom_call" | custom-call | tf_op jit(solution)/shard_map/lanczos/pallas_call | solution.py:596
  104.0 4.4 %finish.1 = (f32[2048,384]{1,0:T(8,128)}, f32[384,256]{1,0:T(8,128)}, f32[384,256]{1,0:T(8,128)}) custom-call(f32[384,2048]{1,0:T(8,128)} %get-tuple-element.7.p, f32[128,384]{1,0:T(8,128)} %get-tuple-element.8.l, f32[384,256]{1,0:T(8,128)} %get-tuple-element.9.h, f32[384,256]{1,0:T(8,128)} %get-tuple-element.10.f), custom_call_target="tpu_custom_call" | custom-call | tf_op jit(solution)/shard_map/finish/pallas_call | solution.py:611

commit v6 on v5

--- a/solution.py
+++ b/solution.py
@@ -17,6 +17,7 @@
 NN = (((1,), (0,)), ((), ()))
 NT = (((1,), (1,)), ((), ()))
 TN = (((0,), (0,)), ((), ()))
+FAR_FIRST = ((2, 1), (2, 0), (1, 1), (3, 1), (0, 1), (1, 0), (3, 0))
 
 
 def halves(a):
@@ -119,6 +120,15 @@
     def row_peer(k):
         return lax.rem(r + k, 8)
 
+    def row_at(d):
+        return 2 * lax.rem(lax.div(r, 2) + d[0], 4) + lax.rem(lax.rem(r, 2) + d[1], 2)
+
+    def chip_at(d):
+        return 4 * lax.rem(lax.div(chip, 4) + d[1], 2) + lax.rem(lax.rem(chip, 4) + d[0], 4)
+
+    def back(d):
+        return ((4 - d[0]) % 4, d[1])
+
     def col_peer(k):
         return lax.rem(c + k, 16)
 
@@ -171,11 +181,11 @@
     def _():
         pl.semaphore_wait(barrier, 24)
 
-    def rs1_send(k):
-        to = row_peer(k)
+    def rs1_send(to):
         remote(stp.at[to], rs1.at[r], rs1_s.at[0], rs1_r.at[0], (to, c)).start()
 
-    loop(1, 8, rs1_send)
+    for d in FAR_FIRST:
+        rs1_send(row_at(d))
 
     def split(i):
         high, rest = halves(cvm[block(i), :])
@@ -196,8 +206,8 @@
     vcol[:, block(r)] = start
     tsh[0] = start
 
-    def ag1(k):
-        return remote(vcol.at[:, block(r)], vcol.at[:, block(r)], ag1_s.at[0], ag1_r.at[r], (row_peer(k), c))
+    def ag1(to):
+        return remote(vcol.at[:, block(r)], vcol.at[:, block(r)], ag1_s.at[0], ag1_r.at[r], (to, c))
 
 
     def turn(tag, dst, at, dev):
@@ -224,21 +234,21 @@
     def gather_start(buf, tag):
         mine = buf.at[0:B, block(c)]
 
-        def send(k):
-            i = lax.rem(chip + k, 8)
+        def send(i):
             remote(mine, mine, ag_s.at[tag], ag_r.at[tag, chip], (r, 2 * i + core)).start()
 
-        loop(1, 8, send)
+        for d in FAR_FIRST:
+            send(chip_at(d))
         remote(mine, mine, fw_s.at[tag], fw_r.at[tag], (r, partner)).start()
 
     def gather_relay(buf, tag):
-        def relay(k):
-            i = lax.rem(chip + 8 - k, 8)
+        def relay(i):
             got = buf.at[0:B, block(2 * i + core)]
             remote(got, got, ag_s.at[tag], ag_r.at[tag, i], (r, c)).wait_recv()
             remote(got, got, fw_s.at[tag], fw_r.at[tag], (r, partner)).start()
 
-        loop(1, 8, relay)
+        for d in FAR_FIRST:
+            relay(chip_at(back(d)))
 
     def gather_all(buf, n, ssem, rsem, tag):
         got = buf.at[0:B, pl.ds(0, n * B)]
@@ -251,8 +261,9 @@
         gather_all(buf, 7, ag_s, fw_r, tag).wait_send()
         gather_all(buf, 8, fw_s, fw_r, tag).wait_send()
 
-    def spread(out, at, n_peers, ssem, rsem, dev):
-        loop(1, n_peers, lambda k: remote(out.at[at], out.at[at], ssem, rsem, dev(k)).start())
+    def spread(out, at, n_peers, ssem, rsem, devices):
+        for dev in devices():
+            remote(out.at[at], out.at[at], ssem, rsem, dev).start()
 
     def rest(out, n_peers, ssem, rsem):
         got = out.at[pl.ds(0, n_peers - 1)]
@@ -261,11 +272,12 @@
     def collect(out, n_peers, ssem, rsem):
         rest(out, n_peers, ssem, rsem).wait_recv()
 
-    def over_row(k):
-        return (row_peer(k), c)
-
-    def over_col(k):
-        return (r, col_peer(k))
+    def over_row():
+        return [(row_at(d), c) for d in FAR_FIRST]
+
+    def over_col():
+        far = [(r, 2 * chip_at(d) + o) for d in FAR_FIRST for o in (core, 1 - core)]
+        return far + [(r, partner)]
 
     wides = {1: (xa1, xb1, xc1, xd1), 3: (xa3, xb3, xc3, xd3)}
 
@@ -273,11 +285,10 @@
         a, b = wides[tag][:2]
         a[...] = value.reshape(8, 16, B)
 
-        def send(k):
-            to = row_peer(k)
+        for d in FAR_FIRST:
+            to = row_at(d)
             remote(a.at[to], b.at[r], sa_s.at[tag], sa_r.at[tag], (to, c)).start()
 
-        loop(1, 8, send)
 
     def wide_second(tag):
         a, b, d = wides[tag][:3]
@@ -298,7 +309,8 @@
         return e[...].reshape(B, B)
 
     turn_start(0, st)
-    loop(1, 8, lambda k: ag1(k).start())
+    for d in FAR_FIRST:
+        ag1(row_at(d)).start()
     turn_wait(0, st)
     gather_start(st, 0)
     def cat(i):
@@ -308,12 +320,13 @@
 
     cat(r)
 
-    def ag1_wait(k):
-        i = lax.rem(r + 8 - k, 8)
+    def ag1_wait(i):
         remote(vcol.at[:, block(i)], vcol.at[:, block(i)], ag1_s.at[0], ag1_r.at[i], (r, c)).wait_recv()
         cat(i)
 
-    loop(1, 8, ag1_wait)
+    for d in FAR_FIRST:
+        ag1_wait(row_at(back(d)))
+
 
     ga[c] = fine(vcol[pl.ds(pl.multiple_of(r * 16, 16), 16), :], vcol[...], NT)
     spread(ga, c, 16, sb_s.at[0], sb_r.at[0], over_col)
@@ -327,13 +340,18 @@
     def across(h):
         return remote(ypart.at[pl.ds(h * 4, 4)], d2d.at[pl.ds(h * 4, 4)], d2d_s.at[h], d2d_r.at[h], (r, partner))
 
-    def theirs(h):
+    def half_at(n):
+        return lax.rem(lax.div(chip, 4) + 1 + n, 2)
+
+    def theirs(n):
+        h = half_at(n)
         ypart[pl.ds(h * 4, 4)] = times(h * 4, 1 - core)
         across(h).start()
 
     loop(0, 2, theirs)
 
-    def ours(h):
+    def ours(n):
+        h = half_at(n)
         yown[pl.ds(h * 4, 4)] = times(h * 4, core)
 
     loop(0, 2, ours)
@@ -341,10 +359,11 @@
     def rs2_copy(i):
         return remote(yown.at[i], rs2.at[chip], rs2_s.at[0], rs2_r.at[0], (r, 2 * i + core))
 
-    def combine(h):
+    def combine(n):
+        h = half_at(n)
         across(h).wait_recv()
-        for t in range(4):
-            i = h * 4 + t
+        for t in (2, 1, 3, 0):
+            i = h * 4 + lax.rem(lax.rem(chip, 4) + t, 4)
             yown[i] = yown[i] + d2d[i]
 
             @pl.when(i != chip)
@@ -441,7 +460,7 @@
         remote(tsh.at[2], tsh.at[3], t_s.at[2], t_r.at[2], origin).start()
 
     def times_t(k):
-        q = lax.rem(lax.div(r, 2) + 1 + k, 4)
+        q = lax.rem(lax.div(r, 2) + jnp.where(k == 0, 2, jnp.where(k == 1, 1, jnp.where(k == 2, 3, 0))), 4)
         o = pl.ds(pl.multiple_of(q * 256, 256), 256)
         a = chi[:, :, :, o].reshape(ROWS, 256)
         b = clo[:, :, :, o].reshape(ROWS, 256)
@@ -449,8 +468,8 @@
         half = full[:B, :] + (full[B:, :] + jnp.dot(wt[0:B, :], b, preferred_element_type=F32))
         y1p[2 * q] = half[:, :B]
         y1p[2 * q + 1] = half[:, B:]
-        for t in range(2):
-            to = 2 * q + t
+        for t in (1, 0):
+            to = 2 * q + lax.rem(lax.rem(r, 2) + t, 2)
 
             @pl.when(to != r)
             def _():

time: 109 us -> 106 us (0.972)
  Pallas kernels: 108 us -> 105 us
    pallas_call x1, Pallas kernels: 103 us -> 101 us  [local(): pl.pallas_call(kernel, out_shape=(jax.ShapeDtypeStruct((3 * B, ROWS), F32...]
where the time goes in v6:
time: 106 us
  Pallas kernels  105 us (99%)
    pallas_call x1, Pallas kernels, local(): pl.pallas_call(kernel, out_shape=(jax.ShapeDtypeStruct((3 * B, ROWS), F32...  101 us
    pallas_call x1, Pallas kernels, local(): pl.pallas_call(finish, grid=(2,), out_shape=(jax.ShapeDtypeStruct((ROWS,...  4.41 us

profile of v6, /device:TPU:1, one launch (start us, length us, event | category | flops | bytes accessed | tf_op | source)
XLA Modules:
  0.0 106.0 jit_solution(9467723265144053903)
XLA Ops:
  0.6 100.9 %lanczos.1 = (f32[384,2048]{1,0:T(8,128)}, f32[128,384]{1,0:T(8,128)}, f32[384,256]{1,0:T(8,128)}, f32[384,256]{1,0:T(8,128)}) custom-call(s32[128]{0:T(128)} %seed.1, f32[2048,1024]{1,0:T(8,128)} %cov.1), custom_call_target="tpu_custom_call" | custom-call | tf_op jit(solution)/shard_map/lanczos/pallas_call | solution.py:615
  101.6 4.4 %finish.1 = (f32[2048,384]{1,0:T(8,128)}, f32[384,256]{1,0:T(8,128)}, f32[384,256]{1,0:T(8,128)}) custom-call(f32[384,2048]{1,0:T(8,128)} %get-tuple-element.7.p, f32[128,384]{1,0:T(8,128)} %get-tuple-element.8.l, f32[384,256]{1,0:T(8,128)} %get-tuple-element.9.h, f32[384,256]{1,0:T(8,128)} %get-tuple-element.10.f), custom_call_target="tpu_custom_call" | custom-call | tf_op jit(solution)/shard_map/finish/pallas_call | solution.py:630

commit v7 on v6

--- a/solution.py
+++ b/solution.py
@@ -502,8 +502,8 @@
     projection[0:B, 0:B] = h1 + h2
     factor_start(sums[B : 2 * B, :] - exact(h2t, h2), aug)
     factor_half(aug, low1, 0)
+    factor_half(aug, low1, 1)
     wide_third(3)
-    factor_half(aug, low1, 1)
     projection[B : 2 * B, 0:B] = low1[:, :B]
     inv1 = low1[:, B:]
     tail = exact(inv1, h2t)

time: 106 us -> 106 us (level)
  no operation moved by 1% of the time
where the time goes in v7:
time: 106 us
  Pallas kernels  105 us (99%)
    pallas_call x1, Pallas kernels, local(): pl.pallas_call(kernel, out_shape=(jax.ShapeDtypeStruct((3 * B, ROWS), F32...  101 us
    pallas_call x1, Pallas kernels, local(): pl.pallas_call(finish, grid=(2,), out_shape=(jax.ShapeDtypeStruct((ROWS,...  4.41 us

profile of v7, /device:TPU:1, one launch (start us, length us, event | category | flops | bytes accessed | tf_op | source)
XLA Modules:
  0.0 106.0 jit_solution(14501855226914243144)
XLA Ops:
  0.6 100.9 %lanczos.1 = (f32[384,2048]{1,0:T(8,128)}, f32[128,384]{1,0:T(8,128)}, f32[384,256]{1,0:T(8,128)}, f32[384,256]{1,0:T(8,128)}) custom-call(s32[128]{0:T(128)} %seed.1, f32[2048,1024]{1,0:T(8,128)} %cov.1), custom_call_target="tpu_custom_call" | custom-call | tf_op jit(solution)/shard_map/lanczos/pallas_call | solution.py:615
  101.5 4.4 %finish.1 = (f32[2048,384]{1,0:T(8,128)}, f32[384,256]{1,0:T(8,128)}, f32[384,256]{1,0:T(8,128)}) custom-call(f32[384,2048]{1,0:T(8,128)} %get-tuple-element.7.p, f32[128,384]{1,0:T(8,128)} %get-tuple-element.8.l, f32[384,256]{1,0:T(8,128)} %get-tuple-element.9.h, f32[384,256]{1,0:T(8,128)} %get-tuple-element.10.f), custom_call_target="tpu_custom_call" | custom-call | tf_op jit(solution)/shard_map/finish/pallas_call | solution.py:630
